TPU v7x, 16 devices: a whole 2x2x2 slice. The times are simulated.
16 devices in a mesh: col: 2 (over z), row: 8 (over y, x, core).
Axes of the slice: x: 2, y: 2, z: 2, core: 2. Of those that a mesh axis runs over, the one named last changes fastest.
Arguments:
- trans_mat: bfloat16 [24576, 24576], P('row', 'col')
- x_start: float32 [24576, 256], P(('col', 'row'))
- teleport: float32 [24576, 256], P(('col', 'row'))
- dangling: int32 [24576], P(('col', 'row'))
Outputs:
- output: float32 [24576, 256], P(('col', 'row'))
All inputs are finite; a program needn't handle non-finite values.
Results may differ from a plain program's by a relative error of at most 0.001.
Values are sent between devices in bfloat16 or wider.
A program may use at most 1 GiB of HBM per device.

v0:
```python
import jax
import jax.numpy as jnp
from jax import lax
from jax.sharding import PartitionSpec as P

SWEEPS = 8
DAMPING = 0.85


def solution(mesh):
    row_size = mesh.shape['row']
    col_size = mesh.shape['col']
    realign = [(col_idx * row_size + row_idx, row_idx * col_size + col_idx)
               for row_idx in range(row_size) for col_idx in range(col_size)]

    def local_sweeps(mat_tile, x_piece, tele_piece, dang_piece):
        vertex_count = mat_tile.shape[1] * col_size
        dang_col = dang_piece.astype(jnp.float32)[:, None]
        x_cur = x_piece
        for sweep_idx in range(SWEEPS):
            dang_mass = lax.psum(jnp.sum(dang_col * x_cur, axis=0), ('col', 'row')) / vertex_count
            x_src = lax.all_gather(x_cur.astype(jnp.bfloat16), 'row', axis=0, tiled=True)
            part_prod = jnp.dot(mat_tile, x_src, preferred_element_type=jnp.float32)
            folded = lax.psum_scatter(part_prod, 'col', scatter_dimension=0, tiled=True)
            aligned = lax.ppermute(folded, ('col', 'row'), perm=realign)
            x_cur = DAMPING * aligned + (DAMPING * dang_mass + (1.0 - DAMPING))[None, :] * tele_piece
        return x_cur

    vec_spec = P(('col', 'row'), None)
    return jax.shard_map(local_sweeps, mesh=mesh,
                         in_specs=(P('row', 'col'), vec_spec, vec_spec, P(('col', 'row'))),
                         out_specs=vec_spec, check_vma=False)
```

profile of v0, /device:TPU:1, one launch (start us, length us, event | category | flops | bytes accessed | tf_op | source)
XLA Modules:
  0.0 1343.7 jit_solution(16764670415982855287)
XLA Ops:
  10.5 43.8 %all-gather.9.cloned.1.call-done = bf16[12288,256]{1,0:T(8,128)(2,1)} async-done(((bf16[1536,256]{1,0:T(8,128)(2,1)}), bf16[12288,256]{1,0:T(8,128)(2,1)}) %all-gather.9.cloned.1.call-update) | async-done | bytes 6291472 | tf_op jit(solution)/shard_map/all_gather | solution.py:22
  86.1 40.9 %reduce-scatter.9.cloned.1.call-done = f32[1536,256]{1,0:T(8,128)} async-done(((f32[3072,256]{1,0:T(8,128)}), f32[1536,256]{1,0:T(8,128)}) %reduce-scatter.9.cloned.1.call-update) | async-done | bytes 1572880 | tf_op jit(solution)/shard_map/reduce_scatter | solution.py:24
  130.9 44.3 %psum.56 = f32[256]{0:T(256)S(1)} all-reduce(f32[256]{0:T(256)S(1)} %get-tuple-element.20), channel_id=1, replica_groups=mesh['col'=2,'row'=8] {'col','row'}, use_global_device_ids=true, to_apply=%region_2.0 | all-reduce | flops 256 | bytes 2048 | tf_op jit(solution)/shard_map/psum | solution.py:21
  176.6 43.5 %all-gather.11.cloned.1.call-done = bf16[12288,256]{1,0:T(8,128)(2,1)} async-done(((bf16[1536,256]{1,0:T(8,128)(2,1)}), bf16[12288,256]{1,0:T(8,128)(2,1)}) %all-gather.11.cloned.1.call-update) | async-done | bytes 6291472 | tf_op jit(solution)/shard_map/all_gather | solution.py:22
  251.9 40.9 %reduce-scatter.11.cloned.1.call-done = f32[1536,256]{1,0:T(8,128)} async-done(((f32[3072,256]{1,0:T(8,128)}), f32[1536,256]{1,0:T(8,128)}) %reduce-scatter.11.cloned.1.call-update) | async-done | bytes 1572880 | tf_op jit(solution)/shard_map/reduce_scatter | solution.py:24
  296.7 44.3 %psum.57 = f32[256]{0:T(256)S(1)} all-reduce(f32[256]{0:T(256)S(1)} %get-tuple-element.18), channel_id=1, replica_groups=mesh['col'=2,'row'=8] {'col','row'}, use_global_device_ids=true, to_apply=%region_5.0 | all-reduce | flops 256 | bytes 2048 | tf_op jit(solution)/shard_map/psum | solution.py:21
  342.5 43.3 %all-gather.13.cloned.1.call-done = bf16[12288,256]{1,0:T(8,128)(2,1)} async-done(((bf16[1536,256]{1,0:T(8,128)(2,1)}), bf16[12288,256]{1,0:T(8,128)(2,1)}) %all-gather.13.cloned.1.call-update) | async-done | bytes 6291472 | tf_op jit(solution)/shard_map/all_gather | solution.py:22
  417.6 40.9 %reduce-scatter.13.cloned.1.call-done = f32[1536,256]{1,0:T(8,128)} async-done(((f32[3072,256]{1,0:T(8,128)}), f32[1536,256]{1,0:T(8,128)}) %reduce-scatter.13.cloned.1.call-update) | async-done | bytes 1572880 | tf_op jit(solution)/shard_map/reduce_scatter | solution.py:24
  462.4 44.3 %psum.58 = f32[256]{0:T(256)S(1)} all-reduce(f32[256]{0:T(256)S(1)} %get-tuple-element.16), channel_id=1, replica_groups=mesh['col'=2,'row'=8] {'col','row'}, use_global_device_ids=true, to_apply=%region_8.0 | all-reduce | flops 256 | bytes 2048 | tf_op jit(solution)/shard_map/psum | solution.py:21
  508.0 43.5 %all-gather.15.cloned.1.call-done = bf16[12288,256]{1,0:T(8,128)(2,1)} async-done(((bf16[1536,256]{1,0:T(8,128)(2,1)}), bf16[12288,256]{1,0:T(8,128)(2,1)}) %all-gather.15.cloned.1.call-update) | async-done | bytes 6291472 | tf_op jit(solution)/shard_map/all_gather | solution.py:22
  583.3 40.9 %reduce-scatter.15.cloned.1.call-done = f32[1536,256]{1,0:T(8,128)} async-done(((f32[3072,256]{1,0:T(8,128)}), f32[1536,256]{1,0:T(8,128)}) %reduce-scatter.15.cloned.1.call-update) | async-done | bytes 1572880 | tf_op jit(solution)/shard_map/reduce_scatter | solution.py:24
  628.1 44.3 %psum.59 = f32[256]{0:T(256)S(1)} all-reduce(f32[256]{0:T(256)S(1)} %get-tuple-element.14), channel_id=1, replica_groups=mesh['col'=2,'row'=8] {'col','row'}, use_global_device_ids=true, to_apply=%region_11.0 | all-reduce | flops 256 | bytes 2048 | tf_op jit(solution)/shard_map/psum | solution.py:21
  674.0 43.3 %all-gather.17.cloned.1.call-done = bf16[12288,256]{1,0:T(8,128)(2,1)} async-done(((bf16[1536,256]{1,0:T(8,128)(2,1)}), bf16[12288,256]{1,0:T(8,128)(2,1)}) %all-gather.17.cloned.1.call-update) | async-done | bytes 6291472 | tf_op jit(solution)/shard_map/all_gather | solution.py:22
  749.1 40.9 %reduce-scatter.17.cloned.1.call-done = f32[1536,256]{1,0:T(8,128)} async-done(((f32[3072,256]{1,0:T(8,128)}), f32[1536,256]{1,0:T(8,128)}) %reduce-scatter.17.cloned.1.call-update) | async-done | bytes 1572880 | tf_op jit(solution)/shard_map/reduce_scatter | solution.py:24
  793.8 44.3 %psum.60 = f32[256]{0:T(256)S(1)} all-reduce(f32[256]{0:T(256)S(1)} %get-tuple-element.12), channel_id=1, replica_groups=mesh['col'=2,'row'=8] {'col','row'}, use_global_device_ids=true, to_apply=%region_14.0 | all-reduce | flops 256 | bytes 2048 | tf_op jit(solution)/shard_map/psum | solution.py:21
  839.5 43.5 %all-gather.19.cloned.1.call-done = bf16[12288,256]{1,0:T(8,128)(2,1)} async-done(((bf16[1536,256]{1,0:T(8,128)(2,1)}), bf16[12288,256]{1,0:T(8,128)(2,1)}) %all-gather.19.cloned.1.call-update) | async-done | bytes 6291472 | tf_op jit(solution)/shard_map/all_gather | solution.py:22
  914.8 40.9 %reduce-scatter.19.cloned.1.call-done = f32[1536,256]{1,0:T(8,128)} async-done(((f32[3072,256]{1,0:T(8,128)}), f32[1536,256]{1,0:T(8,128)}) %reduce-scatter.19.cloned.1.call-update) | async-done | bytes 1572880 | tf_op jit(solution)/shard_map/reduce_scatter | solution.py:24
  959.6 44.3 %psum.61 = f32[256]{0:T(256)S(1)} all-reduce(f32[256]{0:T(256)S(1)} %get-tuple-element.10), channel_id=1, replica_groups=mesh['col'=2,'row'=8] {'col','row'}, use_global_device_ids=true, to_apply=%region_17.0 | all-reduce | flops 256 | bytes 2048 | tf_op jit(solution)/shard_map/psum | solution.py:21
  1005.5 43.2 %all-gather.21.cloned.1.call-done = bf16[12288,256]{1,0:T(8,128)(2,1)} async-done(((bf16[1536,256]{1,0:T(8,128)(2,1)}), bf16[12288,256]{1,0:T(8,128)(2,1)}) %all-gather.21.cloned.1.call-update) | async-done | bytes 6291472 | tf_op jit(solution)/shard_map/all_gather | solution.py:22
  1080.5 40.9 %reduce-scatter.21.cloned.1.call-done = f32[1536,256]{1,0:T(8,128)} async-done(((f32[3072,256]{1,0:T(8,128)}), f32[1536,256]{1,0:T(8,128)}) %reduce-scatter.21.cloned.1.call-update) | async-done | bytes 1572880 | tf_op jit(solution)/shard_map/reduce_scatter | solution.py:24
  1125.3 44.3 %psum.62 = f32[256]{0:T(256)S(1)} all-reduce(f32[256]{0:T(256)S(1)} %get-tuple-element.8), channel_id=1, replica_groups=mesh['col'=2,'row'=8] {'col','row'}, use_global_device_ids=true, to_apply=%region_20.0 | all-reduce | flops 256 | bytes 2048 | tf_op jit(solution)/shard_map/psum | solution.py:21
  1171.0 43.5 %all-gather.23.cloned.1.call-done = bf16[12288,256]{1,0:T(8,128)(2,1)} async-done(((bf16[1536,256]{1,0:T(8,128)(2,1)}), bf16[12288,256]{1,0:T(8,128)(2,1)}) %all-gather.23.cloned.1.call-update) | async-done | bytes 6291472 | tf_op jit(solution)/shard_map/all_gather | solution.py:22
  1246.2 40.9 %reduce-scatter.23.cloned.1.call-done = f32[1536,256]{1,0:T(8,128)} async-done(((f32[3072,256]{1,0:T(8,128)}), f32[1536,256]{1,0:T(8,128)}) %reduce-scatter.23.cloned.1.call-update) | async-done | bytes 1572880 | tf_op jit(solution)/shard_map/reduce_scatter | solution.py:24
  1291.1 44.3 %psum.63 = f32[256]{0:T(256)S(1)} all-reduce(f32[256]{0:T(256)S(1)} %get-tuple-element.5), channel_id=1, replica_groups=mesh['col'=2,'row'=8] {'col','row'}, use_global_device_ids=true, to_apply=%region_23.0 | all-reduce | flops 256 | bytes 2048 | tf_op jit(solution)/shard_map/psum | solution.py:21
  (76 shorter events, 300.5 us)
Async XLA Ops:
  6.5 47.8 %all-gather.9.cloned.1.call-start = ((), (), s32[]{:S(2)}) async-start(), calls=%async_computation.8 | async-start | bytes 7077888 | tf_op jit(solution)/shard_map/all_gather | solution.py:22
  10.5 116.5 %reduce-scatter.9.cloned.1.call-start = ((), (), s32[]{:S(2)}) async-start(), calls=%async_computation.9 | async-start | bytes 4718592 | tf_op jit(solution)/shard_map/reduce_scatter | solution.py:24
  86.1 134.0 %all-gather.11.cloned.1.call-start = ((), (), s32[]{:S(2)}) async-start(), calls=%async_computation.10 | async-start | bytes 7077888 | tf_op jit(solution)/shard_map/all_gather | solution.py:22
  127.0 48.2 %collective-permute-start = (f32[1536,256]{1,0:T(8,128)}, f32[1536,256]{1,0:T(8,128)S(1)}, u32[]{:S(2)}, u32[]{:S(2)}) collective-permute-start(f32[1536,256]{1,0:T(8,128)} %reduce-scatter.9.cloned.1.call-done), channel_id=1, source_target_pairs={{0,0},{8,1},{1,2},{9,3},{2,4},{10,5},{3,6},{11,7},{4,8},{12,9},{5,... | collective-permute-start | bytes 4718600 | tf_op jit(solution)/shard_map/ppermute | solution.py:25
  176.5 116.2 %reduce-scatter.11.cloned.1.call-start = ((), (), s32[]{:S(2)}) async-start(), calls=%async_computation.11 | async-start | bytes 4718592 | tf_op jit(solution)/shard_map/reduce_scatter | solution.py:24
  251.8 134.0 %all-gather.13.cloned.1.call-start = ((), (), s32[]{:S(2)}) async-start(), calls=%async_computation.12 | async-start | bytes 7077888 | tf_op jit(solution)/shard_map/all_gather | solution.py:22
  292.7 48.2 %collective-permute-start.1 = (f32[1536,256]{1,0:T(8,128)}, f32[1536,256]{1,0:T(8,128)S(1)}, u32[]{:S(2)}, u32[]{:S(2)}) collective-permute-start(f32[1536,256]{1,0:T(8,128)} %reduce-scatter.11.cloned.1.call-done), channel_id=1, source_target_pairs={{0,0},{8,1},{1,2},{9,3},{2,4},{10,5},{3,6},{11,7},{4,8},{12,9},{5,... | collective-permute-start | bytes 4718600 | tf_op jit(solution)/shard_map/ppermute | solution.py:25
  342.2 116.2 %reduce-scatter.13.cloned.1.call-start = ((), (), s32[]{:S(2)}) async-start(), calls=%async_computation.13 | async-start | bytes 4718592 | tf_op jit(solution)/shard_map/reduce_scatter | solution.py:24
  417.6 134.0 %all-gather.15.cloned.1.call-start = ((), (), s32[]{:S(2)}) async-start(), calls=%async_computation.14 | async-start | bytes 7077888 | tf_op jit(solution)/shard_map/all_gather | solution.py:22
  458.5 48.2 %collective-permute-start.2 = (f32[1536,256]{1,0:T(8,128)}, f32[1536,256]{1,0:T(8,128)S(1)}, u32[]{:S(2)}, u32[]{:S(2)}) collective-permute-start(f32[1536,256]{1,0:T(8,128)} %reduce-scatter.13.cloned.1.call-done), channel_id=1, source_target_pairs={{0,0},{8,1},{1,2},{9,3},{2,4},{10,5},{3,6},{11,7},{4,8},{12,9},{5,... | collective-permute-start | bytes 4718600 | tf_op jit(solution)/shard_map/ppermute | solution.py:25
  508.0 116.2 %reduce-scatter.15.cloned.1.call-start = ((), (), s32[]{:S(2)}) async-start(), calls=%async_computation.15 | async-start | bytes 4718592 | tf_op jit(solution)/shard_map/reduce_scatter | solution.py:24
  583.3 134.0 %all-gather.17.cloned.1.call-start = ((), (), s32[]{:S(2)}) async-start(), calls=%async_computation.16 | async-start | bytes 7077888 | tf_op jit(solution)/shard_map/all_gather | solution.py:22
  624.2 48.2 %collective-permute-start.3 = (f32[1536,256]{1,0:T(8,128)}, f32[1536,256]{1,0:T(8,128)S(1)}, u32[]{:S(2)}, u32[]{:S(2)}) collective-permute-start(f32[1536,256]{1,0:T(8,128)} %reduce-scatter.15.cloned.1.call-done), channel_id=1, source_target_pairs={{0,0},{8,1},{1,2},{9,3},{2,4},{10,5},{3,6},{11,7},{4,8},{12,9},{5,... | collective-permute-start | bytes 4718600 | tf_op jit(solution)/shard_map/ppermute | solution.py:25
  673.7 116.3 %reduce-scatter.17.cloned.1.call-start = ((), (), s32[]{:S(2)}) async-start(), calls=%async_computation.17 | async-start | bytes 4718592 | tf_op jit(solution)/shard_map/reduce_scatter | solution.py:24
  749.0 134.0 %all-gather.19.cloned.1.call-start = ((), (), s32[]{:S(2)}) async-start(), calls=%async_computation.18 | async-start | bytes 7077888 | tf_op jit(solution)/shard_map/all_gather | solution.py:22
  790.0 48.2 %collective-permute-start.4 = (f32[1536,256]{1,0:T(8,128)}, f32[1536,256]{1,0:T(8,128)S(1)}, u32[]{:S(2)}, u32[]{:S(2)}) collective-permute-start(f32[1536,256]{1,0:T(8,128)} %reduce-scatter.17.cloned.1.call-done), channel_id=1, source_target_pairs={{0,0},{8,1},{1,2},{9,3},{2,4},{10,5},{3,6},{11,7},{4,8},{12,9},{5,... | collective-permute-start | bytes 4718600 | tf_op jit(solution)/shard_map/ppermute | solution.py:25
  839.4 116.2 %reduce-scatter.19.cloned.1.call-start = ((), (), s32[]{:S(2)}) async-start(), calls=%async_computation.19 | async-start | bytes 4718592 | tf_op jit(solution)/shard_map/reduce_scatter | solution.py:24
  914.7 134.0 %all-gather.21.cloned.1.call-start = ((), (), s32[]{:S(2)}) async-start(), calls=%async_computation.20 | async-start | bytes 7077888 | tf_op jit(solution)/shard_map/all_gather | solution.py:22
  955.7 48.2 %collective-permute-start.5 = (f32[1536,256]{1,0:T(8,128)}, f32[1536,256]{1,0:T(8,128)S(1)}, u32[]{:S(2)}, u32[]{:S(2)}) collective-permute-start(f32[1536,256]{1,0:T(8,128)} %reduce-scatter.19.cloned.1.call-done), channel_id=1, source_target_pairs={{0,0},{8,1},{1,2},{9,3},{2,4},{10,5},{3,6},{11,7},{4,8},{12,9},{5,... | collective-permute-start | bytes 4718600 | tf_op jit(solution)/shard_map/ppermute | solution.py:25
  1005.2 116.2 %reduce-scatter.21.cloned.1.call-start = ((), (), s32[]{:S(2)}) async-start(), calls=%async_computation.21 | async-start | bytes 4718592 | tf_op jit(solution)/shard_map/reduce_scatter | solution.py:24
  1080.5 134.0 %all-gather.23.cloned.1.call-start = ((), (), s32[]{:S(2)}) async-start(), calls=%async_computation.22 | async-start | bytes 7077888 | tf_op jit(solution)/shard_map/all_gather | solution.py:22
  1121.4 48.2 %collective-permute-start.6 = (f32[1536,256]{1,0:T(8,128)}, f32[1536,256]{1,0:T(8,128)S(1)}, u32[]{:S(2)}, u32[]{:S(2)}) collective-permute-start(f32[1536,256]{1,0:T(8,128)} %reduce-scatter.21.cloned.1.call-done), channel_id=1, source_target_pairs={{0,0},{8,1},{1,2},{9,3},{2,4},{10,5},{3,6},{11,7},{4,8},{12,9},{5,... | collective-permute-start | bytes 4718600 | tf_op jit(solution)/shard_map/ppermute | solution.py:25
  1170.9 116.2 %reduce-scatter.23.cloned.1.call-start = ((), (), s32[]{:S(2)}) async-start(), calls=%async_computation.23 | async-start | bytes 4718592 | tf_op jit(solution)/shard_map/reduce_scatter | solution.py:24
  1287.1 48.2 %collective-permute-start.7 = (f32[1536,256]{1,0:T(8,128)}, f32[1536,256]{1,0:T(8,128)S(1)}, u32[]{:S(2)}, u32[]{:S(2)}) collective-permute-start(f32[1536,256]{1,0:T(8,128)} %reduce-scatter.23.cloned.1.call-done), channel_id=1, source_target_pairs={{0,0},{8,1},{1,2},{9,3},{2,4},{10,5},{3,6},{11,7},{4,8},{12,9},{5,... | collective-permute-start | bytes 4718600 | tf_op jit(solution)/shard_map/ppermute | solution.py:25
  (1 other events, 89.2 us)
Sparse Core Ops, SparseCore 0:
  10.6 43.6 all-gather.8
  86.2 40.7 reduce-scatter.8
  176.6 43.3 all-gather.10
  251.9 40.7 reduce-scatter.10
  342.4 43.3 all-gather.12
  417.7 40.7 reduce-scatter.12
  508.1 43.3 all-gather.14
  583.4 40.7 reduce-scatter.14
  673.8 43.3 all-gather.16
  749.1 40.7 reduce-scatter.16
  839.6 43.3 all-gather.18
  914.9 40.7 reduce-scatter.18
  1005.3 43.3 all-gather.20
  1080.6 40.7 reduce-scatter.20
  1171.0 43.3 all-gather.22
  1246.3 40.7 reduce-scatter.22
where the time goes:
time: 1360 us; the launch traced here: 1340 us
  waiting for transfers between devices  675 us (50%)
  blocking collectives  355 us (26%)
  matrix products  254 us (19%)
  starting transfers between devices  32.4 us (2%)
  other arithmetic  13.9 us (1%)
  between operations  13.8 us (1%)
    psum x8, blocking collectives, local_sweeps(): lax.psum(jnp.sum(dang_col * x_cur, axis=0), ('col', 'row')) / vertex_count  355 us
    all_gather x8, waiting for transfers between devices, local_sweeps(): lax.all_gather(x_cur.astype(jnp.bfloat16), 'row', axis=0, tiled=True)  348 us
    reduce_scatter x8, waiting for transfers between devices, local_sweeps(): folded = lax.psum_scatter(part_prod, 'col', scatter_dimension=0, tiled=True)  327 us
    dot_general x8, matrix products, local_sweeps(): part_prod = jnp.dot(mat_tile, x_src, preferred_element_type=jnp.float32)  254 us
    ppermute x8, starting transfers between devices, local_sweeps(): aligned = lax.ppermute(folded, ('col', 'row'), perm=realign)  31.2 us
  transfers between devices with their start and end apart: 24, of which 16 were waited for; matrix products, arithmetic and copies ran while one was open for 0% of the time, Pallas kernels for 0%

commit v1 on v0

v1 whole, which is shorter than its diff:
```python
import functools

import jax
import jax.numpy as jnp
from jax import lax
from jax.experimental import pallas as pl
from jax.experimental.pallas import tpu as pltpu
from jax.sharding import PartitionSpec as P

SWEEPS = 8
DAMPING = 0.85
CH = 128
LAG = 4
SLOTS = 3
MT = 512
MB = 256
MESH = pl.DeviceIdType.MESH


def sweeps_kernel(steps, a_ref, x0_ref, v_ref, dang_ref, s0_ref, o_ref,
                  abuf, xbuf, xst, yacc, zr, spart, sbuf, svec,
                  a_sem, x0_sem, z_send, z_recv, r_send, r_recv, y_send, y_recv, x_send, x_recv,
                  d1_send, d1_recv, d2_send, d2_recv, s_send, s_recv):
    i = lax.axis_index('row')
    z = lax.axis_index('col')
    y, x, c = i // 4, (i // 2) % 2, i % 2
    me = z * 8 + i
    home = z == y
    away = z != y
    part = jnp.where(home, 0, 1)
    k_own = 2 * x + c
    k_sib = 2 * x + 1 - c
    k_x = 2 * (1 - x) + c
    k_d = 2 * (1 - x) + 1 - c
    z_dev = {'col': 1 - z, 'row': i}
    sib_dev = {'col': z, 'row': i + 1 - 2 * c}
    x_dev = {'col': z, 'row': i + 2 - 4 * x}
    y_dev = {'col': z, 'row': i + 4 - 8 * y}
    piece = steps * CH
    vertices = 16 * piece

    def other(off):
        dev = (me + off) % 16
        return {'col': dev // 8, 'row': dev % 8}, dev

    barrier = pltpu.get_barrier_semaphore()

    @pl.loop(1, 16)
    def _(off):
        dev, _ = other(off)
        pl.semaphore_signal(barrier, inc=1, device_id=dev, device_id_type=MESH)

    pl.semaphore_wait(barrier, 15)

    def remote(src, dst, send, recv, dev):
        return pltpu.make_async_remote_copy(src_ref=src, dst_ref=dst, send_sem=send, recv_sem=recv,
                                            device_id=dev, device_id_type=MESH)

    def z_copy(t, q):
        rows = pl.ds(pl.multiple_of((1 - part) * piece + q * CH, CH), CH)
        return remote(yacc.at[t, rows], zr.at[t, pl.ds(pl.multiple_of(q * CH, CH), CH)],
                      z_send.at[t, q], z_recv.at[t, q], z_dev)

    def r_copy(p, q):
        return remote(xst.at[p, q], xbuf.at[p, q, k_own, 1], r_send.at[p, q], r_recv.at[p, q], z_dev)

    def y_copy(p, q):
        return remote(xbuf.at[p, q, k_own], xbuf.at[p, q, k_own], y_send.at[p, q], y_recv.at[p, q], y_dev)

    def x_copy(p, q):
        return remote(xbuf.at[p, q, k_own], xbuf.at[p, q, k_own], x_send.at[p, q], x_recv.at[p, q], x_dev)

    def d1_copy(p, q):
        return remote(xbuf.at[p, q, k_own], xbuf.at[p, q, k_own], d1_send.at[p, q], d1_recv.at[p, q], sib_dev)

    def d2_copy(p, q):
        return remote(xbuf.at[p, q, k_x], xbuf.at[p, q, k_x], d2_send.at[p, q], d2_recv.at[p, q], sib_dev)

    def landed(ref, sem):
        pltpu.make_async_copy(ref, ref, sem).wait()

    def a_start(g):
        q = lax.rem(g, steps)
        slot = lax.rem(g, SLOTS)
        for b in range(8):
            cols = pl.ds(pl.multiple_of(b * piece + q * CH, CH), CH)
            pltpu.make_async_copy(a_ref.at[:, cols], abuf.at[slot, :, pl.ds(b * CH, CH)], a_sem.at[slot]).start()

    def a_next(g):
        @pl.when(g + SLOTS < SWEEPS * steps)
        def _():
            a_start(g + SLOTS)

    def block_x(p, q):
        return xbuf[p, q].reshape(8 * CH, xbuf.shape[-1])

    def multiply(p, q, g):
        slot = lax.rem(g, SLOTS)
        landed(abuf.at[slot], a_sem.at[slot])

        @pl.loop(0, 2 * piece // MT)
        def _(m):
            rows = pl.ds(pl.multiple_of(m * MT, MT), MT)
            yacc[p, rows] += jnp.dot(abuf[slot, rows], block_x(p, q), preferred_element_type=jnp.float32)

        a_next(g)

    def multiply_last(p, g):
        slot = lax.rem(g, SLOTS)
        landed(abuf.at[slot], a_sem.at[slot])
        x_last = block_x(p, steps - 1)

        @pl.loop(0, piece // MB)
        def _(m):
            for which in (1 - part, part):
                rows = pl.ds(pl.multiple_of(which * piece + m * MB, MB), MB)
                yacc[p, rows] += jnp.dot(abuf[slot, rows], x_last, preferred_element_type=jnp.float32)

            @pl.when(m == 0)
            def _():
                z_copy(p, 0).start()
                z_copy(p, 1).start()

        a_next(g)

    def clear(p):
        @pl.loop(0, 2 * piece // MB)
        def _(m):
            rows = pl.ds(pl.multiple_of(m * MB, MB), MB)
            yacc[p, rows] = jnp.zeros((MB, yacc.shape[-1]), jnp.float32)

    def new_rows(t, q):
        rows = pl.ds(pl.multiple_of(q * CH, CH), CH)
        mine = pl.ds(pl.multiple_of(part * piece + q * CH, CH), CH)
        landed(zr.at[t, rows], z_recv.at[t, q])
        return DAMPING * (yacc[t, mine] + zr[t, rows]) + svec[0:1] * v_ref[rows], rows

    @pl.loop(0, SLOTS)
    def _(g):
        a_start(g)

    @pl.loop(0, steps)
    def _(q):
        pltpu.make_async_copy(x0_ref.at[:, :, q], xbuf.at[0, q], x0_sem.at[q]).start()

    svec[...] = jnp.broadcast_to(DAMPING * s0_ref[...] + (1.0 - DAMPING), svec.shape)
    clear(0)

    @pl.loop(0, steps - 1)
    def _(q):
        landed(xbuf.at[0, q], x0_sem.at[q])
        multiply(0, q, q)

    landed(xbuf.at[0, steps - 1], x0_sem.at[steps - 1])
    multiply_last(0, steps - 1)

    @pl.loop(0, SWEEPS - 1)
    def _(sweep):
        t = lax.rem(sweep, 2)
        p = 1 - t

        @pl.when(sweep > 0)
        def _():
            @pl.loop(1, 16)
            def _(off):
                _, dev = other(off)
                landed(sbuf.at[t, dev], s_recv.at[t, dev])

            s_sum = jnp.sum(sbuf[t].reshape(16 * 8, sbuf.shape[-1]), axis=0, keepdims=True) / vertices
            svec[...] = jnp.broadcast_to(DAMPING * s_sum + (1.0 - DAMPING), svec.shape)

        clear(p)
        spart[p] = jnp.zeros(spart.shape[1:], jnp.float32)

        @pl.loop(0, steps + LAG)
        def _(step):
            @pl.when(step + 2 < steps)
            def _():
                z_copy(t, step + 2).start()

            @pl.when(step < steps)
            def _():
                q = step
                rows_new, rows = new_rows(t, q)
                rows_bf = rows_new.astype(jnp.bfloat16)

                @pl.when(home)
                def _():
                    xbuf[p, q, k_own, 0] = rows_bf

                @pl.when(away)
                def _():
                    xst[p, q] = rows_bf

                spart[p] += jnp.sum((dang_ref[rows] * rows_new).reshape(CH // 8, 8, rows_new.shape[-1]), axis=0)

                @pl.when(away)
                def _():
                    r_copy(p, q).start()

            @pl.when(step == steps - 1)
            def _():
                sbuf[p, me] = spart[p]

                @pl.loop(1, 16)
                def _(off):
                    dev, _ = other(off)
                    remote(spart.at[p], sbuf.at[p, me], s_send.at[p, off], s_recv.at[p, me], dev).start()

            @pl.when((step >= 1) & (step < steps + 1) & home)
            def _():
                q = step - 1
                landed(xst.at[p, q], r_recv.at[p, q])
                y_copy(p, q).start()
                x_copy(p, q).start()
                d1_copy(p, q).start()

            @pl.when((step >= 2) & (step < steps + 2) & away)
            def _():
                q = step - 2
                landed(xbuf.at[p, q, k_own], y_recv.at[p, q])
                x_copy(p, q).start()
                d1_copy(p, q).start()

            @pl.when((step >= 3) & (step < steps + 3))
            def _():
                q = step - 3
                landed(xbuf.at[p, q, k_x], x_recv.at[p, q])
                d2_copy(p, q).start()

            @pl.when(step >= 4)
            def _():
                q = step - 4
                landed(xbuf.at[p, q, k_sib], d1_recv.at[p, q])
                landed(xbuf.at[p, q, k_d], d2_recv.at[p, q])

                @pl.when(q < steps - 1)
                def _():
                    multiply(p, q, (sweep + 1) * steps + q)

        multiply_last(p, (sweep + 1) * steps + steps - 1)

        @pl.loop(0, steps)
        def _(q):
            z_copy(t, q).wait_send()
            x_copy(p, q).wait_send()
            d1_copy(p, q).wait_send()
            d2_copy(p, q).wait_send()

            @pl.when(home)
            def _():
                y_copy(p, q).wait_send()

            @pl.when(away)
            def _():
                r_copy(p, q).wait_send()

        @pl.loop(1, 16)
        def _(off):
            dev, _ = other(off)
            remote(spart.at[p], sbuf.at[p, me], s_send.at[p, off], s_recv.at[p, me], dev).wait_send()

    t = (SWEEPS - 1) % 2

    @pl.loop(1, 16)
    def _(off):
        _, dev = other(off)
        landed(sbuf.at[t, dev], s_recv.at[t, dev])

    s_sum = jnp.sum(sbuf[t].reshape(16 * 8, sbuf.shape[-1]), axis=0, keepdims=True) / vertices
    svec[...] = jnp.broadcast_to(DAMPING * s_sum + (1.0 - DAMPING), svec.shape)

    @pl.loop(0, steps)
    def _(q):
        @pl.when(q + 2 < steps)
        def _():
            z_copy(t, q + 2).start()

        rows_new, rows = new_rows(t, q)
        o_ref[rows] = rows_new

    @pl.loop(0, steps)
    def _(q):
        z_copy(t, q).wait_send()


def solution(mesh):
    def piece_of(dev):
        z, i = dev // 8, dev % 8
        return 2 * i + (0 if z == i // 4 else 1)

    to_sums = [(piece_of(dev), dev) for dev in range(16)]
    from_sums = [(dev, piece_of(dev)) for dev in range(16)]

    def local_sweeps(mat_tile, x_piece, tele_piece, dang_piece):
        piece, vecs = x_piece.shape
        steps = piece // CH
        vertex_count = 16 * piece
        dang_col = dang_piece.astype(jnp.float32)[:, None]
        s0 = lax.psum(jnp.sum(dang_col * x_piece, axis=0, keepdims=True), ('col', 'row')) / vertex_count
        x_src = lax.all_gather(x_piece.astype(jnp.bfloat16), 'row', axis=0, tiled=True)
        x_src = x_src.reshape(4, 2, steps, CH, vecs)
        tele = lax.ppermute(tele_piece, ('col', 'row'), perm=to_sums)
        dang = lax.ppermute(dang_piece, ('col', 'row'), perm=to_sums).astype(jnp.float32)[:, None]
        sems = pltpu.SemaphoreType.DMA
        out = pl.pallas_call(
            functools.partial(sweeps_kernel, steps),
            out_shape=jax.ShapeDtypeStruct((piece, vecs), jnp.float32),
            in_specs=[pl.BlockSpec(memory_space=pl.ANY), pl.BlockSpec(memory_space=pl.ANY)]
            + [pl.BlockSpec(memory_space=pltpu.VMEM)] * 3,
            out_specs=pl.BlockSpec(memory_space=pltpu.VMEM),
            scratch_shapes=[
                pltpu.VMEM((SLOTS, 2 * piece, 8 * CH), jnp.bfloat16),
                pltpu.VMEM((2, steps, 4, 2, CH, vecs), jnp.bfloat16),
                pltpu.VMEM((2, steps, CH, vecs), jnp.bfloat16),
                pltpu.VMEM((2, 2 * piece, vecs), jnp.float32),
                pltpu.VMEM((2, piece, vecs), jnp.float32),
                pltpu.VMEM((2, 8, vecs), jnp.float32),
                pltpu.VMEM((2, 16, 8, vecs), jnp.float32),
                pltpu.VMEM((8, vecs), jnp.float32),
                sems((SLOTS,)), sems((steps,)),
            ] + [sems((2, steps))] * 12 + [sems((2, 16))] * 2,
            compiler_params=pltpu.CompilerParams(collective_id=0, has_side_effects=True,
                                                 vmem_limit_bytes=67_000_000),
            name='sweeps',
        )(mat_tile, x_src, tele, dang, s0)
        return lax.ppermute(out, ('col', 'row'), perm=from_sums)

    vec_spec = P(('col', 'row'), None)
    return jax.shard_map(local_sweeps, mesh=mesh,
                         in_specs=(P('row', 'col'), vec_spec, vec_spec, P(('col', 'row'))),
                         out_specs=vec_spec, check_vma=False)
```

time: 1360 us -> 755 us (0.56); the launches traced: 1340 us -> 754 us
  waiting for transfers between devices: 675 us -> 17.3 us
  Pallas kernels: 0 us -> 588 us
  matrix products: 254 us -> 0 us
  blocking collectives: 355 us -> 115 us
  starting transfers between devices: 32.4 us -> 13.1 us
    pallas_call x0 -> x1, Pallas kernels: none -> 588 us  [local_sweeps(): pl.pallas_call(functools.partial(sweeps_kernel, steps), out_shape=jax.Sha...]
    all_gather x8 -> x1, waiting for transfers between devices: 348 us -> 0.01 us  [local_sweeps(): lax.all_gather(x_piece.astype(jnp.bfloat16), 'row', axis=0, tiled=True)]
    reduce_scatter x8 -> x0, waiting for transfers between devices: 327 us -> none  [local_sweeps(): folded = lax.psum_scatter(part_prod, 'col', scatter_dimension=0, tiled=True)]
    dot_general x8 -> x0, matrix products: 254 us -> none  [local_sweeps(): part_prod = jnp.dot(mat_tile, x_src, preferred_element_type=jnp.float32)]
    psum x8 -> x1, blocking collectives: 355 us -> 115 us  [local_sweeps(): lax.psum(jnp.sum(dang_col * x_piece, axis=0, keepdims=True), ('col', 'row'))]
    ppermute x8 -> x3, starting transfers between devices: 31.2 us -> 13.1 us  [the longest x1 5.12 us: local_sweeps(): return lax.ppermute(out, ('col', 'row'), perm=from_sums)]
    ppermute x8 -> x3, waiting for transfers between devices: 0.02 us -> 17.3 us  [the longest x1 17.3 us: local_sweeps(): return lax.ppermute(out, ('col', 'row'), perm=from_sums)]
  transfers between devices with their start and end apart: 24 -> 4, of which waited for: 16 -> 1; matrix products, arithmetic and copies ran while one was open for 0% -> 0% of each run, Pallas kernels for 0% -> 0%
where the time goes in v1:
time: 755 us; the launch traced here: 754 us
  Pallas kernels  588 us (78%)
  blocking collectives  115 us (15%)
  waiting for transfers between devices  17.3 us (2%)
  between operations  13.5 us (2%)
  starting transfers between devices  13.1 us (2%)
    pallas_call x1, Pallas kernels, local_sweeps(): pl.pallas_call(functools.partial(sweeps_kernel, steps), out_shape=jax.Sha...  588 us
    psum x1, blocking collectives, local_sweeps(): lax.psum(jnp.sum(dang_col * x_piece, axis=0, keepdims=True), ('col', 'row'))  115 us
    ppermute x1, waiting for transfers between devices, local_sweeps(): return lax.ppermute(out, ('col', 'row'), perm=from_sums)  17.3 us
  transfers between devices with their start and end apart: 4, of which 1 were waited for; matrix products, arithmetic and copies ran while one was open for 0% of the time, Pallas kernels for 0%

profile of v1, /device:TPU:1, one launch (start us, length us, event | category | flops | bytes accessed | tf_op | source)
XLA Modules:
  0.0 754.1 jit_solution(16408517014991517962)
XLA Ops:
  6.5 0.0 all-gather.2.cloned.1.call-start
  6.5 0.7 convert_element_type.11
  7.2 0.0 copy-start.1
  7.2 0.0 copy-start
  7.2 3.2 multiply_reduce_fusion
  10.5 0.0 all-gather.2.cloned.1.call-update
  10.5 0.0 copy-done.1
  10.5 4.6 collective-permute-start
  15.1 0.0 copy-done
  15.1 3.4 collective-permute-start.1
  18.5 115.1 %psum.7 = f32[1,256]{1,0:T(1,128)S(1)} all-reduce(f32[1,256]{1,0:T(1,128)S(1)} %bitcast.3), channel_id=1, replica_groups=mesh['col'=2,'row'=8] {'col','row'}, use_global_device_ids=true, to_apply=%region_1.0 | all-reduce | flops 256 | bytes 2048 | tf_op jit(solution)/shard_map/psum | solution.py:300
  133.7 0.5 broadcast_multiply_fusion.s0_ref
  134.2 0.0 collective-permute-done.1
  134.2 1.2 broadcast_in_dim.9.dang_ref
  135.4 0.0 collective-permute-done.v_ref
  135.4 0.0 all-gather.2.cloned.1.call-done
  135.4 588.3 %sweeps.1 = f32[1536,256]{1,0:T(8,128)} custom-call(bf16[3072,12288]{1,0:T(8,128)(2,1)} %a_ref.1, bf16[4,2,12,128,256]{4,3,2,1,0:T(8,128)(2,1)} %bitcast.2, f32[1536,256]{1,0:T(8,128)} %collective-permute-done.v_ref, f32[1536,1]{1,0:T(8,128)} %broadcast_in_dim.9.dang_ref, f32[1,256]{1,0:T(1,128)} %broadcast_multiply_fusion.s0_ref), custom_call_target="tpu_custom_call" | custom-call | tf_op jit(solution)/shard_map/sweeps/pallas_call | solution.py:306
  723.7 5.1 collective-permute-start.2
  728.8 17.3 %collective-permute-done.2 = f32[1536,256]{1,0:T(8,128)S(1)} collective-permute-done((f32[1536,256]{1,0:T(8,128)}, f32[1536,256]{1,0:T(8,128)S(1)}, u32[]{:S(2)}, u32[]{:S(2)}) %collective-permute-start.2) | collective-permute-done | bytes 1572896 | tf_op jit(solution)/shard_map/ppermute | solution.py:327
  746.1 1.1 copy.7
  (1 shorter events, 0.0 us)
Async XLA Ops:
  6.5 128.8 %all-gather.2.cloned.1.call-start = ((), (), s32[]{:S(2)}) async-start(), calls=%async_computation | async-start | bytes 7077888 | tf_op jit(solution)/shard_map/all_gather | solution.py:301
  7.2 3.3 copy-start.1
  7.2 7.9 %copy-start = (s32[1536]{0:T(1024)S(1)}, s32[1536]{0:T(1024)}, u32[]{:S(2)}) copy-start(s32[1536]{0:T(1024)} %param.7) | copy-start | bytes 18436
  10.5 124.9 %collective-permute-start = (f32[1536,256]{1,0:T(8,128)S(1)}, f32[1536,256]{1,0:T(8,128)}, u32[]{:S(2)}, u32[]{:S(2)}) collective-permute-start(f32[1536,256]{1,0:T(8,128)S(1)} %copy-done.1), channel_id=1, source_target_pairs={{0,0},{2,1},{4,2},{6,3},{9,4},{11,5},{13,6},{15,7},{1,8},{3,9},{5,... | collective-permute-start | bytes 4718600 | tf_op jit(solution)/shard_map/ppermute | solution.py:303
  15.1 119.1 %collective-permute-start.1 = (s32[1536]{0:T(1024)S(1)}, s32[1536]{0:T(1024)S(1)}, u32[]{:S(2)}, u32[]{:S(2)}) collective-permute-start(s32[1536]{0:T(1024)S(1)} %copy-done), channel_id=1, source_target_pairs={{0,0},{2,1},{4,2},{6,3},{9,4},{11,5},{13,6},{15,7},{1,8},{3,9},{5,... | collective-permute-start | bytes 18440 | tf_op jit(solution)/shard_map/ppermute | solution.py:304
  723.7 22.4 %collective-permute-start.2 = (f32[1536,256]{1,0:T(8,128)}, f32[1536,256]{1,0:T(8,128)S(1)}, u32[]{:S(2)}, u32[]{:S(2)}) collective-permute-start(f32[1536,256]{1,0:T(8,128)} %sweeps.1), channel_id=1, source_target_pairs={{0,0},{1,2},{2,4},{3,6},{4,9},{5,11},{6,13},{7,15},{8,1},{9,3},{10... | collective-permute-start | bytes 4718600 | tf_op jit(solution)/shard_map/ppermute | solution.py:327
Sparse Core Ops, SparseCore 0:
  10.6 82.1 all-gather.1

commit v2 on v1

v2 whole, which is shorter than its diff:
```python
import jax
import jax.numpy as jnp
from jax import lax
from jax.experimental import pallas as pl
from jax.experimental.pallas import tpu as pltpu
from jax.sharding import PartitionSpec as P

SWEEPS = 8
DAMPING = 0.85
CH = 64
BR = 128
LAG = 2
AHEAD = 3
SLOTS = 3
MT = 512
MB = 256
VAHEAD = 3
MESH = pl.DeviceIdType.MESH


def sweeps_kernel(a_ref, x_ref, v_ref, dang_ref, o_ref,
                  abuf, xbuf, xst, yacc, zr, vperm, dperm, dcol, spart, sbuf, svec,
                  a_sem, g_send, gx_recv, gy_recv, gd_recv, gs_recv, v_send, v_recv, dang_sem, o_send, o_recv,
                  z_send, z_recv, r_send, r_recv, y_send, y_recv, x_send, x_recv,
                  d1_send, d1_recv, d2_send, d2_recv, s_send, s_recv):
    i = lax.axis_index('row')
    z = lax.axis_index('col')
    y, x, c = i // 4, (i // 2) % 2, i % 2
    me = z * 8 + i
    home = z == y
    away = z != y
    part = jnp.where(home, 0, 1)
    k_own = 2 * x + c
    k_sib = 2 * x + 1 - c
    k_x = 2 * (1 - x) + c
    k_d = 2 * (1 - x) + 1 - c
    sib_dev = {'col': z, 'row': i + 1 - 2 * c}
    x_dev = {'col': z, 'row': i + 2 - 4 * x}
    y_row = i + 4 - 8 * y
    y_dev = {'col': z, 'row': y_row}
    z_dev = {'col': 1 - z, 'row': i}
    piece, vecs = o_ref.shape
    chunks = piece // CH
    blocks = piece // BR
    per = BR // CH
    vertices = 16 * piece

    def other(off):
        dev = (me + off) % 16
        return {'col': dev // 8, 'row': dev % 8}, dev

    barrier = pltpu.get_barrier_semaphore()

    @pl.loop(1, 16)
    def _(off):
        dev, _ = other(off)
        pl.semaphore_signal(barrier, inc=1, device_id=dev, device_id_type=MESH)

    def remote(src, dst, send, recv, dev):
        return pltpu.make_async_remote_copy(src_ref=src, dst_ref=dst, send_sem=send, recv_sem=recv,
                                            device_id=dev, device_id_type=MESH)

    def same(ref, send, recv, dev):
        return remote(ref, ref, send, recv, dev)

    def landed(ref, sem):
        pltpu.make_async_copy(ref, ref, sem).wait()

    def at(start, size):
        return pl.ds(pl.multiple_of(start, size), size)

    def both(p, q, k):
        return xbuf.at[p, q // per, k, :, at(q % per * CH, CH)]

    def one(p, q, k, b):
        return xbuf.at[p, q // per, k, b, at(q % per * CH, CH)]

    def z_copy(t, q):
        rows = at((1 - part) * piece + q * CH, CH)
        return remote(yacc.at[t, rows], zr.at[t, at(q * CH, CH)], z_send.at[t, q], z_recv.at[t, q], z_dev)

    def r_copy(p, q):
        row = jnp.where(q % 2 == 0, i, y_row)
        return remote(xst.at[p, q], one(p, q, k_own, 1), r_send.at[p, q], r_recv.at[p, q], {'col': 1 - z, 'row': row})

    def y_copy(p, q, ref):
        return same(ref, y_send.at[p, q], y_recv.at[p, q], y_dev)

    def x_copy(p, q, ref):
        return same(ref, x_send.at[p, q], x_recv.at[p, q], x_dev)

    def d1_copy(p, q, ref):
        return same(ref, d1_send.at[p, q], d1_recv.at[p, q], sib_dev)

    def d2_copy(p, q):
        return same(both(p, q, k_x), d2_send.at[p, q], d2_recv.at[p, q], sib_dev)

    def s_copy(p, off):
        dev, _ = other(off)
        return remote(spart.at[p], sbuf.at[p, me], s_send.at[p, off], s_recv.at[p, me], dev)

    def send_s(p):
        sbuf[p, me] = spart[p]

        @pl.loop(1, 16)
        def _(off):
            s_copy(p, off).start()

    def sum_s(t):
        @pl.loop(1, 16)
        def _(off):
            _, dev = other(off)
            landed(sbuf.at[t, dev], s_recv.at[t, dev])

        s_sum = jnp.sum(sbuf[t].reshape(16 * 8, vecs), axis=0, keepdims=True) / vertices
        svec[...] = jnp.broadcast_to(DAMPING * s_sum + (1.0 - DAMPING), svec.shape)

    def a_start(g):
        q = lax.rem(g, blocks)
        slot = lax.rem(g, SLOTS)
        for b in range(8):
            cols = at(b * piece + q * BR, BR)
            pltpu.make_async_copy(a_ref.at[:, cols], abuf.at[slot, :, pl.ds(b * BR, BR)], a_sem.at[slot]).start()

    def a_next(g):
        @pl.when(g + SLOTS < SWEEPS * blocks)
        def _():
            a_start(g + SLOTS)

    def block_x(p, q):
        return xbuf[p, q].reshape(8 * BR, vecs)

    def multiply(p, q, g):
        slot = lax.rem(g, SLOTS)
        landed(abuf.at[slot], a_sem.at[slot])

        @pl.loop(0, 2 * piece // MT)
        def _(m):
            rows = at(m * MT, MT)
            yacc[p, rows] += jnp.dot(abuf[slot, rows], block_x(p, q), preferred_element_type=jnp.float32)

        a_next(g)

    def multiply_last(p, g):
        slot = lax.rem(g, SLOTS)
        landed(abuf.at[slot], a_sem.at[slot])
        x_last = block_x(p, blocks - 1)

        @pl.loop(0, piece // MB)
        def _(m):
            for which in (1 - part, part):
                rows = at(which * piece + m * MB, MB)
                yacc[p, rows] += jnp.dot(abuf[slot, rows], x_last, preferred_element_type=jnp.float32)

            @pl.when(m == 0)
            def _():
                for q in range(AHEAD):
                    z_copy(p, q).start()

        a_next(g)

    def clear(p):
        @pl.loop(0, 2 * piece // MB)
        def _(m):
            yacc[p, at(m * MB, MB)] = jnp.zeros((MB, vecs), jnp.float32)

    def new_rows(t, q):
        rows = at(q * CH, CH)
        landed(zr.at[t, rows], z_recv.at[t, q])
        return DAMPING * (yacc[t, at(part * piece + q * CH, CH)] + zr[t, rows]) + svec[0:1] * vperm[rows], rows

    def dang_sum(col, rows_f32):
        halves = [col * rows_f32[:, h:h + 128] for h in range(0, vecs, 128)]
        return jnp.sum(jnp.concatenate(halves, axis=1).reshape(-1, 8, vecs), axis=0)

    def dang_col(ref, b):
        return jnp.transpose(jnp.broadcast_to(ref[pl.ds(b, 1)], (BR, 128)))

    @pl.loop(0, SLOTS)
    def _(g):
        a_start(g)

    o_p = 2 * i + part
    o_dev = {'col': o_p // 8, 'row': o_p % 8}
    moves = o_p != me
    stays = o_p == me
    v_row = me // 2
    v_dev = {'col': jnp.where(me % 2 == 0, v_row // 4, 1 - v_row // 4), 'row': v_row}

    def v_copy(b):
        rows = at(b * BR, BR)
        return remote(v_ref.at[rows], vperm.at[rows], v_send.at[b], v_recv.at[b], v_dev)

    dang_copy = remote(dang_ref, dperm, dang_sem.at[0], dang_sem.at[1], v_dev)

    g_own, g_x, g_y, g_d = 2 * y + x, 2 * y + 1 - x, 2 * (1 - y) + x, 2 * (1 - y) + 1 - x
    spart[0] = jnp.zeros(spart.shape[1:], jnp.float32)

    @pl.loop(0, blocks)
    def _(b):
        rows_x = x_ref[at(b * BR, BR)]
        xbuf[0, b, g_own, c] = rows_x.astype(jnp.bfloat16)
        spart[0] += dang_sum(dang_col(dang_ref, b), rows_x)

    pl.semaphore_wait(barrier, 15)

    @pl.when(moves)
    def _():
        dang_copy.start()

    @pl.when(stays)
    def _():
        dperm[...] = dang_ref[...]
        vperm[...] = v_ref[...]

    send_s(0)
    clear(0)

    @pl.loop(0, blocks + 3 * LAG)
    def _(step):
        @pl.when(step < blocks)
        def _():
            own = xbuf.at[0, step, g_own, c]
            same(own, g_send.at[step], gx_recv.at[step], x_dev).start()
            same(own, g_send.at[step], gy_recv.at[step], y_dev).start()
            same(own, g_send.at[step], gs_recv.at[step], sib_dev).start()

        @pl.when((step >= LAG) & (step < blocks + LAG))
        def _():
            b = step - LAG
            from_x, from_y = xbuf.at[0, b, g_x, c], xbuf.at[0, b, g_y, c]
            landed(from_y, gy_recv.at[b])

            @pl.when(b % 2 == 0)
            def _():
                same(from_y, g_send.at[b], gd_recv.at[b], x_dev).start()

            landed(from_x, gx_recv.at[b])

            @pl.when(b % 2 == 1)
            def _():
                same(from_x, g_send.at[b], gd_recv.at[b], y_dev).start()

            same(from_x, g_send.at[b], gs_recv.at[b], sib_dev).start()
            same(from_y, g_send.at[b], gs_recv.at[b], sib_dev).start()

        @pl.when((step >= 2 * LAG) & (step < blocks + 2 * LAG))
        def _():
            b = step - 2 * LAG
            from_d = xbuf.at[0, b, g_d, c]
            landed(from_d, gd_recv.at[b])
            same(from_d, g_send.at[b], gs_recv.at[b], sib_dev).start()

        @pl.when(step >= 3 * LAG)
        def _():
            b = step - 3 * LAG
            landed(xbuf.at[0, b, :, 1 - c], gs_recv.at[b])

            @pl.when(b < blocks - 1)
            def _():
                multiply(0, b, b)

    @pl.when(moves)
    def _():
        for b in range(VAHEAD):
            v_copy(b).start()

    multiply_last(0, blocks - 1)

    @pl.loop(0, blocks)
    def _(b):
        landed(yacc.at[1, pl.ds(0, 7 * BR // 2)], g_send.at[b])

    @pl.loop(1, 16)
    def _(off):
        s_copy(0, off).wait_send()

    @pl.when(moves)
    def _():
        dang_copy.wait()

    @pl.loop(0, blocks)
    def _(b):
        dcol[at(b * BR, BR)] = dang_col(dperm, b)

    @pl.loop(0, SWEEPS - 1)
    def _(sweep):
        t = lax.rem(sweep, 2)
        p = 1 - t
        sum_s(t)
        clear(p)
        spart[p] = jnp.zeros(spart.shape[1:], jnp.float32)

        @pl.loop(0, chunks + 4 * LAG)
        def _(step):
            @pl.when(step + AHEAD < chunks)
            def _():
                z_copy(t, step + AHEAD).start()

            @pl.when(moves & (sweep == 0) & (step < chunks) & (step % per == 0))
            def _():
                b = step // per

                @pl.when(b + VAHEAD < blocks)
                def _():
                    v_copy(b + VAHEAD).start()

                v_copy(b).wait_recv()

            @pl.when(step < chunks)
            def _():
                q = step
                rows_new, rows = new_rows(t, q)
                rows_bf = rows_new.astype(jnp.bfloat16)

                @pl.when(home)
                def _():
                    xbuf[p, q // per, k_own, 0, at(q % per * CH, CH)] = rows_bf

                @pl.when(away)
                def _():
                    xst[p, q] = rows_bf

                spart[p] += dang_sum(dcol[rows], rows_new)

                @pl.when(away)
                def _():
                    r_copy(p, q).start()

            @pl.when(step == chunks - 1)
            def _():
                send_s(p)

            @pl.when((step >= LAG) & (step < chunks + LAG))
            def _():
                q = step - LAG
                even = q % 2 == 0

                def spread(ref):
                    y_copy(p, q, ref).start()
                    x_copy(p, q, ref).start()
                    d1_copy(p, q, ref).start()

                @pl.when(even & home)
                def _():
                    landed(one(p, q, k_own, 1), r_recv.at[p, q])
                    spread(both(p, q, k_own))

                @pl.when(jnp.logical_not(even) & away)
                def _():
                    landed(one(p, q, k_own, 1), r_recv.at[p, q])

                @pl.when(jnp.logical_not(even))
                def _():
                    spread(one(p, q, k_own, part))

            @pl.when((step >= 2 * LAG) & (step < chunks + 2 * LAG))
            def _():
                q = step - 2 * LAG
                even = q % 2 == 0

                @pl.when(even & away)
                def _():
                    ref = both(p, q, k_own)
                    landed(ref, y_recv.at[p, q])
                    x_copy(p, q, ref).start()
                    d1_copy(p, q, ref).start()

                @pl.when(jnp.logical_not(even))
                def _():
                    ref = one(p, q, k_own, 1 - part)
                    landed(ref, y_recv.at[p, q])
                    x_copy(p, q, ref).start()
                    d1_copy(p, q, ref).start()

            @pl.when((step >= 3 * LAG) & (step < chunks + 3 * LAG))
            def _():
                q = step - 3 * LAG
                landed(both(p, q, k_x), x_recv.at[p, q])
                d2_copy(p, q).start()

            @pl.when(step >= 4 * LAG)
            def _():
                q = step - 4 * LAG
                landed(both(p, q, k_sib), d1_recv.at[p, q])
                landed(both(p, q, k_d), d2_recv.at[p, q])
                b = q // per

                @pl.when((q % per == per - 1) & (b < blocks - 1))
                def _():
                    multiply(p, b, (sweep + 1) * blocks + b)

        multiply_last(p, (sweep + 1) * blocks + blocks - 1)

        @pl.loop(0, chunks)
        def _(q):
            even = q % 2 == 0
            z_copy(t, q).wait_send()
            landed(both(p, q, k_own), x_send.at[p, q])
            landed(both(p, q, k_own), d1_send.at[p, q])
            d2_copy(p, q).wait_send()

            @pl.when(even & home)
            def _():
                landed(both(p, q, k_own), y_send.at[p, q])

            @pl.when(jnp.logical_not(even))
            def _():
                landed(one(p, q, k_own, part), y_send.at[p, q])

            @pl.when(away)
            def _():
                r_copy(p, q).wait_send()

        @pl.loop(1, 16)
        def _(off):
            s_copy(p, off).wait_send()

    t = (SWEEPS - 1) % 2

    def o_copy(q):
        rows = at(q * CH, CH)
        return remote(zr.at[t, rows], o_ref.at[rows], o_send.at[q], o_recv.at[q], o_dev)

    sum_s(t)

    @pl.loop(0, chunks)
    def _(q):
        @pl.when(q + AHEAD < chunks)
        def _():
            z_copy(t, q + AHEAD).start()

        rows_new, rows = new_rows(t, q)

        @pl.when(moves)
        def _():
            zr[t, rows] = rows_new
            o_copy(q).start()

        @pl.when(stays)
        def _():
            o_ref[rows] = rows_new

    @pl.loop(0, chunks)
    def _(q):
        z_copy(t, q).wait_send()

        @pl.when(moves)
        def _():
            o_copy(q).wait()

    @pl.when(moves)
    def _():
        @pl.loop(0, blocks)
        def _(b):
            v_copy(b).wait_send()


def solution(mesh):
    def local_sweeps(mat_tile, x_piece, tele_piece, dang_piece):
        piece, vecs = x_piece.shape
        chunks, blocks = piece // CH, piece // BR
        dang_rows = dang_piece.astype(jnp.float32).reshape(blocks, 128)
        sems = pltpu.SemaphoreType.DMA
        return pl.pallas_call(
            sweeps_kernel,
            out_shape=jax.ShapeDtypeStruct((piece, vecs), jnp.float32),
            in_specs=[pl.BlockSpec(memory_space=pl.ANY)] + [pl.BlockSpec(memory_space=pltpu.VMEM)] * 3,
            out_specs=pl.BlockSpec(memory_space=pltpu.VMEM),
            scratch_shapes=[
                pltpu.VMEM((SLOTS, 2 * piece, 8 * BR), jnp.bfloat16),
                pltpu.VMEM((2, blocks, 4, 2, BR, vecs), jnp.bfloat16),
                pltpu.VMEM((2, chunks, CH, vecs), jnp.bfloat16),
                pltpu.VMEM((2, 2 * piece, vecs), jnp.float32),
                pltpu.VMEM((2, piece, vecs), jnp.float32),
                pltpu.VMEM((piece, vecs), jnp.float32),
                pltpu.VMEM((blocks, 128), jnp.float32),
                pltpu.VMEM((piece, 128), jnp.float32),
                pltpu.VMEM((2, 8, vecs), jnp.float32),
                pltpu.VMEM((2, 16, 8, vecs), jnp.float32),
                pltpu.VMEM((8, vecs), jnp.float32),
                sems((SLOTS,)),
            ] + [sems((blocks,))] * 7 + [sems((2,))] + [sems((chunks,))] * 2 + [sems((2, chunks))] * 12
            + [sems((2, 16))] * 2,
            compiler_params=pltpu.CompilerParams(collective_id=0, has_side_effects=True,
                                                 vmem_limit_bytes=67_000_000),
            name='sweeps',
        )(mat_tile, x_piece, tele_piece, dang_rows)

    vec_spec = P(('col', 'row'), None)
    return jax.shard_map(local_sweeps, mesh=mesh,
                         in_specs=(P('row', 'col'), vec_spec, vec_spec, P(('col', 'row'))),
                         out_specs=vec_spec, check_vma=False)
```

time: 755 us -> 588 us (0.78)
  blocking collectives: 115 us -> 0 us
  waiting for transfers between devices: 17.3 us -> 0 us
  between operations: 13.5 us -> 0.01 us
  starting transfers between devices: 13.1 us -> 0 us
    psum x1 -> x0, blocking collectives: 115 us -> none  [local_sweeps(): lax.psum(jnp.sum(dang_col * x_piece, axis=0, keepdims=True), ('col', 'row'))]
    ppermute x3 -> x0, waiting for transfers between devices: 17.3 us -> none  [the longest x1 17.3 us: local_sweeps(): return lax.ppermute(out, ('col', 'row'), perm=from_sums)]
    ppermute x3 -> x0, starting transfers between devices: 13.1 us -> none  [the longest x1 5.12 us: local_sweeps(): return lax.ppermute(out, ('col', 'row'), perm=from_sums)]
  transfers between devices with their start and end apart: 4 -> 0, of which waited for: 1 -> 0; matrix products, arithmetic and copies ran while one was open for 0% -> 0% of each run, Pallas kernels for 0% -> 0%
where the time goes in v2:
time: 588 us
  Pallas kernels  584 us (99%)
    pallas_call x1, Pallas kernels, local_sweeps(): pl.pallas_call(sweeps_kernel, out_shape=jax.ShapeDtypeStruct((piece, vecs...  584 us

profile of v2, /device:TPU:1, one launch (start us, length us, event | category | flops | bytes accessed | tf_op | source)
XLA Modules:
  0.0 587.6 jit_solution(5557386003666417949)
XLA Ops:
  0.0 1.3 convert_bitcast_fusion.dang_ref
  1.3 583.7 %sweeps.1 = f32[1536,256]{1,0:T(8,128)} custom-call(bf16[3072,12288]{1,0:T(8,128)(2,1)} %a_ref.1, f32[1536,256]{1,0:T(8,128)} %x_ref.1, f32[1536,256]{1,0:T(8,128)} %v_ref.1, f32[12,128]{1,0:T(8,128)} %convert_bitcast_fusion.dang_ref), custom_call_target="tpu_custom_call" | custom-call | tf_op jit(solution)/shard_map/sweeps/pallas_call | solution.py:465
  585.0 2.7 copy.6

commit v3 on v2

--- a/solution.py
+++ b/solution.py
@@ -7,10 +7,15 @@
 
 SWEEPS = 8
 DAMPING = 0.85
-CH = 64
+CH = 32
 BR = 128
+AHEAD = 4
+TAIL = 4
+RELAY, BACK, BACK_RELAYED, OVER_Y, OVER_Y_RELAYED, OVER_X, OVER_X_RELAYED, HERE, HERE_RELAYED = 4, 6, 10, 10, 14, 14, 17, 16, 19
+DRAIN = 17
+SENT = 20
 LAG = 2
-AHEAD = 3
+FINAL_RELAY = 6
 SLOTS = 3
 MT = 512
 MB = 256
@@ -19,9 +24,9 @@
 
 
 def sweeps_kernel(a_ref, x_ref, v_ref, dang_ref, o_ref,
-                  abuf, xbuf, xst, yacc, zr, vperm, dperm, dcol, spart, sbuf, svec,
-                  a_sem, g_send, gx_recv, gy_recv, gd_recv, gs_recv, v_send, v_recv, dang_sem, o_send, o_recv,
-                  z_send, z_recv, r_send, r_recv, y_send, y_recv, x_send, x_recv,
+                  abuf, xbuf, xst, rst, yacc, zr, vperm, dperm, dcol, spart, sbuf, svec,
+                  a_sem, g_send, gx_recv, gy_recv, gd_recv, gs_recv, v_send, v_recv, dang_sem, o_send, o_recv, f_send, f_recv,
+                  z_send, z_recv, r_send, r_recv, t_send, t_recv, y_send, y_recv, x_send, x_recv,
                   d1_send, d1_recv, d2_send, d2_recv, s_send, s_recv):
     i = lax.axis_index('row')
     z = lax.axis_index('col')
@@ -79,9 +84,20 @@
         rows = at((1 - part) * piece + q * CH, CH)
         return remote(yacc.at[t, rows], zr.at[t, at(q * CH, CH)], z_send.at[t, q], z_recv.at[t, q], z_dev)
 
+    def relayed(q):
+        return (q % 2 == 0) & (q < chunks - TAIL)
+
+    def direct(q):
+        return jnp.logical_not(relayed(q))
+
     def r_copy(p, q):
-        row = jnp.where(q % 2 == 0, i, y_row)
-        return remote(xst.at[p, q], one(p, q, k_own, 1), r_send.at[p, q], r_recv.at[p, q], {'col': 1 - z, 'row': row})
+        return remote(xst.at[p, q], one(p, q, k_own, 1), r_send.at[p, q], r_recv.at[p, q], z_dev)
+
+    def to_relay(p, q):
+        return remote(xst.at[p, q], rst.at[p, q // 2], r_send.at[p, q], t_recv.at[p, q // 2], y_dev)
+
+    def from_relay(p, q):
+        return remote(rst.at[p, q // 2], one(p, q, k_own, 1), t_send.at[p, q // 2], r_recv.at[p, q], z_dev)
 
     def y_copy(p, q, ref):
         return same(ref, y_send.at[p, q], y_recv.at[p, q], y_dev)
@@ -130,16 +146,23 @@
     def block_x(p, q):
         return xbuf[p, q].reshape(8 * BR, vecs)
 
-    def multiply(p, q, g):
+    def multiply(p, b, g, k):
         slot = lax.rem(g, SLOTS)
-        landed(abuf.at[slot], a_sem.at[slot])
+
+        @pl.when(k == 0)
+        def _():
+            landed(abuf.at[slot], a_sem.at[slot])
+
+        x_k = xbuf[p, b, k].reshape(2 * BR, vecs)
 
         @pl.loop(0, 2 * piece // MT)
         def _(m):
             rows = at(m * MT, MT)
-            yacc[p, rows] += jnp.dot(abuf[slot, rows], block_x(p, q), preferred_element_type=jnp.float32)
-
-        a_next(g)
+            yacc[p, rows] += jnp.dot(abuf[slot, rows, at(k * 2 * BR, 2 * BR)], x_k, preferred_element_type=jnp.float32)
+
+        @pl.when(k == 3)
+        def _():
+            a_next(g)
 
     def multiply_last(p, g):
         slot = lax.rem(g, SLOTS)
@@ -258,7 +281,8 @@
 
             @pl.when(b < blocks - 1)
             def _():
-                multiply(0, b, b)
+                for k in range(4):
+                    multiply(0, b, b, k)
 
     @pl.when(moves)
     def _():
@@ -288,129 +312,162 @@
         t = lax.rem(sweep, 2)
         p = 1 - t
         sum_s(t)
-        clear(p)
         spart[p] = jnp.zeros(spart.shape[1:], jnp.float32)
 
-        @pl.loop(0, chunks + 4 * LAG)
-        def _(step):
-            @pl.when(step + AHEAD < chunks)
-            def _():
-                z_copy(t, step + AHEAD).start()
-
-            @pl.when(moves & (sweep == 0) & (step < chunks) & (step % per == 0))
-            def _():
-                b = step // per
-
-                @pl.when(b + VAHEAD < blocks)
-                def _():
-                    v_copy(b + VAHEAD).start()
-
-                v_copy(b).wait_recv()
-
-            @pl.when(step < chunks)
-            def _():
-                q = step
-                rows_new, rows = new_rows(t, q)
-                rows_bf = rows_new.astype(jnp.bfloat16)
-
-                @pl.when(home)
-                def _():
-                    xbuf[p, q // per, k_own, 0, at(q % per * CH, CH)] = rows_bf
-
-                @pl.when(away)
-                def _():
-                    xst[p, q] = rows_bf
-
-                spart[p] += dang_sum(dcol[rows], rows_new)
-
-                @pl.when(away)
-                def _():
-                    r_copy(p, q).start()
-
-            @pl.when(step == chunks - 1)
-            def _():
-                send_s(p)
-
-            @pl.when((step >= LAG) & (step < chunks + LAG))
-            def _():
-                q = step - LAG
-                even = q % 2 == 0
-
-                def spread(ref):
-                    y_copy(p, q, ref).start()
-                    x_copy(p, q, ref).start()
-                    d1_copy(p, q, ref).start()
-
-                @pl.when(even & home)
-                def _():
-                    landed(one(p, q, k_own, 1), r_recv.at[p, q])
-                    spread(both(p, q, k_own))
-
-                @pl.when(jnp.logical_not(even) & away)
-                def _():
-                    landed(one(p, q, k_own, 1), r_recv.at[p, q])
-
-                @pl.when(jnp.logical_not(even))
-                def _():
-                    spread(one(p, q, k_own, part))
-
-            @pl.when((step >= 2 * LAG) & (step < chunks + 2 * LAG))
-            def _():
-                q = step - 2 * LAG
-                even = q % 2 == 0
-
-                @pl.when(even & away)
-                def _():
-                    ref = both(p, q, k_own)
-                    landed(ref, y_recv.at[p, q])
-                    x_copy(p, q, ref).start()
-                    d1_copy(p, q, ref).start()
-
-                @pl.when(jnp.logical_not(even))
-                def _():
-                    ref = one(p, q, k_own, 1 - part)
-                    landed(ref, y_recv.at[p, q])
-                    x_copy(p, q, ref).start()
-                    d1_copy(p, q, ref).start()
-
-            @pl.when((step >= 3 * LAG) & (step < chunks + 3 * LAG))
-            def _():
-                q = step - 3 * LAG
-                landed(both(p, q, k_x), x_recv.at[p, q])
-                d2_copy(p, q).start()
-
-            @pl.when(step >= 4 * LAG)
-            def _():
-                q = step - 4 * LAG
-                landed(both(p, q, k_sib), d1_recv.at[p, q])
-                landed(both(p, q, k_d), d2_recv.at[p, q])
-                b = q // per
-
-                @pl.when((q % per == per - 1) & (b < blocks - 1))
-                def _():
-                    multiply(p, b, (sweep + 1) * blocks + b)
-
-        multiply_last(p, (sweep + 1) * blocks + blocks - 1)
-
-        @pl.loop(0, chunks)
-        def _(q):
-            even = q % 2 == 0
+        def spread(q, ref):
+            y_copy(p, q, ref).start()
+            x_copy(p, q, ref).start()
+            d1_copy(p, q, ref).start()
+
+        def forward(q, ref):
+            landed(ref, y_recv.at[p, q])
+            x_copy(p, q, ref).start()
+            d1_copy(p, q, ref).start()
+
+        def sent(q):
             z_copy(t, q).wait_send()
             landed(both(p, q, k_own), x_send.at[p, q])
             landed(both(p, q, k_own), d1_send.at[p, q])
             d2_copy(p, q).wait_send()
 
-            @pl.when(even & home)
+            @pl.when(away)
+            def _():
+                r_copy(p, q).wait_send()
+
+            @pl.when(direct(q) & home)
             def _():
                 landed(both(p, q, k_own), y_send.at[p, q])
 
-            @pl.when(jnp.logical_not(even))
+            @pl.when(relayed(q))
             def _():
                 landed(one(p, q, k_own, part), y_send.at[p, q])
 
-            @pl.when(away)
-            def _():
-                r_copy(p, q).wait_send()
+            @pl.when(relayed(q) & home)
+            def _():
+                from_relay(p, q).wait_send()
+
+        @pl.loop(0, chunks + DRAIN)
+        def _(step):
+            def chunk(lag, where):
+                q = step - lag
+                return q, (q >= 0) & (q < chunks) & where(q)
+
+            @pl.when(step + AHEAD < chunks)
+            def _():
+                z_copy(t, step + AHEAD).start()
+
+            @pl.when(moves & (sweep == 0) & (step < chunks) & (step % per == 0))
+            def _():
+                b = step // per
+
+                @pl.when(b + VAHEAD < blocks)
+                def _():
+                    v_copy(b + VAHEAD).start()
+
+                v_copy(b).wait_recv()
+
+            @pl.when(step < chunks)
+            def _():
+                q = step
+                rows_new, rows = new_rows(t, q)
+                rows_bf = rows_new.astype(jnp.bfloat16)
+
+                @pl.when(home)
+                def _():
+                    xbuf[p, q // per, k_own, 0, at(q % per * CH, CH)] = rows_bf
+
+                @pl.when(away)
+                def _():
+                    xst[p, q] = rows_bf
+
+                spart[p] += dang_sum(dcol[rows], rows_new)
+
+                @pl.when(away & relayed(q))
+                def _():
+                    to_relay(p, q).start()
+
+                @pl.when(away & direct(q))
+                def _():
+                    r_copy(p, q).start()
+
+            @pl.when(step == chunks - 1)
+            def _():
+                send_s(p)
+
+            q, on = chunk(RELAY, relayed)
+
+            @pl.when(on & home)
+            def _():
+                landed(rst.at[p, q // 2], t_recv.at[p, q // 2])
+                from_relay(p, q).start()
+                spread(q, one(p, q, k_own, 0))
+
+            q, on = chunk(BACK, direct)
+
+            @pl.when(on & home)
+            def _():
+                landed(one(p, q, k_own, 1), r_recv.at[p, q])
+                spread(q, both(p, q, k_own))
+
+            q, on = chunk(OVER_Y, direct)
+
+            @pl.when(on & away)
+            def _():
+                forward(q, both(p, q, k_own))
+
+            q, on = chunk(BACK_RELAYED, relayed)
+
+            @pl.when(on & away)
+            def _():
+                forward(q, one(p, q, k_own, 0))
+                landed(one(p, q, k_own, 1), r_recv.at[p, q])
+                spread(q, one(p, q, k_own, 1))
+
+            q, on = chunk(OVER_Y_RELAYED, relayed)
+
+            @pl.when(on & home)
+            def _():
+                forward(q, one(p, q, k_own, 1))
+
+            for lag, where in ((OVER_X, direct), (OVER_X_RELAYED, relayed)):
+                q, on = chunk(lag, where)
+
+                @pl.when(on)
+                def _(q=q):
+                    landed(both(p, q, k_x), x_recv.at[p, q])
+                    d2_copy(p, q).start()
+
+            for lag, where in ((HERE, direct), (HERE_RELAYED, relayed)):
+                q, on = chunk(lag, where)
+
+                @pl.when(on)
+                def _(q=q):
+                    landed(both(p, q, k_sib), d1_recv.at[p, q])
+                    landed(both(p, q, k_d), d2_recv.at[p, q])
+
+            @pl.when(step == per)
+            def _():
+                clear(p)
+
+            turn = step - HERE_RELAYED - per // 2
+            b = turn // per
+
+            @pl.when((turn >= 0) & (b < blocks - 1))
+            def _():
+                for k in range(4 // per):
+                    multiply(p, b, (sweep + 1) * blocks + b, turn % per * (4 // per) + k)
+
+            q, on = chunk(SENT, lambda q: True)
+
+            @pl.when(on)
+            def _():
+                sent(q)
+
+        multiply_last(p, (sweep + 1) * blocks + blocks - 1)
+
+        @pl.loop(chunks + DRAIN - SENT, chunks)
+        def _(q):
+            sent(q)
 
         @pl.loop(1, 16)
         def _(off):
@@ -422,24 +479,51 @@
         rows = at(q * CH, CH)
         return remote(zr.at[t, rows], o_ref.at[rows], o_send.at[q], o_recv.at[q], o_dev)
 
+    def o_to_relay(q):
+        rows = at(q * CH, CH)
+        return remote(zr.at[t, rows], zr.at[1 - t, rows], o_send.at[q], f_recv.at[q], y_dev)
+
+    def o_from_relay(q):
+        rows = at(q * CH, CH)
+        dev = 2 * y_row + 1
+        return remote(zr.at[1 - t, rows], o_ref.at[rows], f_send.at[q], o_recv.at[q],
+                      {'col': dev // 8, 'row': dev % 8})
+
     sum_s(t)
 
-    @pl.loop(0, chunks)
-    def _(q):
-        @pl.when(q + AHEAD < chunks)
-        def _():
-            z_copy(t, q + AHEAD).start()
-
-        rows_new, rows = new_rows(t, q)
-
-        @pl.when(moves)
-        def _():
-            zr[t, rows] = rows_new
-            o_copy(q).start()
-
-        @pl.when(stays)
-        def _():
-            o_ref[rows] = rows_new
+    @pl.loop(0, chunks + FINAL_RELAY)
+    def _(step):
+        @pl.when(step + AHEAD < chunks)
+        def _():
+            z_copy(t, step + AHEAD).start()
+
+        @pl.when(step < chunks)
+        def _():
+            rows_new, rows = new_rows(t, step)
+
+            @pl.when(moves)
+            def _():
+                zr[t, rows] = rows_new
+
+            @pl.when(away & relayed(step))
+            def _():
+                o_to_relay(step).start()
+
+            @pl.when(moves & (home | direct(step)))
+            def _():
+                o_copy(step).start()
+
+            @pl.when(stays)
+            def _():
+                o_ref[rows] = rows_new
+
+        q = step - FINAL_RELAY
+
+        @pl.when((q >= 0) & relayed(q) & home)
+        def _():
+            rows = at(q * CH, CH)
+            landed(zr.at[1 - t, rows], f_recv.at[q])
+            o_from_relay(q).start()
 
     @pl.loop(0, chunks)
     def _(q):
@@ -448,6 +532,10 @@
         @pl.when(moves)
         def _():
             o_copy(q).wait()
+
+        @pl.when(relayed(q) & home)
+        def _():
+            o_from_relay(q).wait_send()
 
     @pl.when(moves)
     def _():
@@ -471,6 +559,7 @@
                 pltpu.VMEM((SLOTS, 2 * piece, 8 * BR), jnp.bfloat16),
                 pltpu.VMEM((2, blocks, 4, 2, BR, vecs), jnp.bfloat16),
                 pltpu.VMEM((2, chunks, CH, vecs), jnp.bfloat16),
+                pltpu.VMEM((2, chunks // 2, CH, vecs), jnp.bfloat16),
                 pltpu.VMEM((2, 2 * piece, vecs), jnp.float32),
                 pltpu.VMEM((2, piece, vecs), jnp.float32),
                 pltpu.VMEM((piece, vecs), jnp.float32),
@@ -480,7 +569,8 @@
                 pltpu.VMEM((2, 16, 8, vecs), jnp.float32),
                 pltpu.VMEM((8, vecs), jnp.float32),
                 sems((SLOTS,)),
-            ] + [sems((blocks,))] * 7 + [sems((2,))] + [sems((chunks,))] * 2 + [sems((2, chunks))] * 12
+            ] + [sems((blocks,))] * 7 + [sems((2,))] + [sems((chunks,))] * 4 + [sems((2, chunks))] * 4
+            + [sems((2, chunks // 2))] * 2 + [sems((2, chunks))] * 8
             + [sems((2, 16))] * 2,
             compiler_params=pltpu.CompilerParams(collective_id=0, has_side_effects=True,
                                                  vmem_limit_bytes=67_000_000),

time: 588 us -> 856 us (1.46)
  Pallas kernels: 584 us -> 852 us
    pallas_call x1, Pallas kernels: 584 us -> 852 us  [local_sweeps(): pl.pallas_call(sweeps_kernel, out_shape=jax.ShapeDtypeStruct((piece, vecs...]
where the time goes in v3:
time: 856 us
  Pallas kernels  852 us (100%)
    pallas_call x1, Pallas kernels, local_sweeps(): pl.pallas_call(sweeps_kernel, out_shape=jax.ShapeDtypeStruct((piece, vecs...  852 us

profile of v3, /device:TPU:1, one launch (start us, length us, event | category | flops | bytes accessed | tf_op | source)
XLA Modules:
  0.0 856.1 jit_solution(3139411642891193048)
XLA Ops:
  0.0 1.3 convert_bitcast_fusion.dang_ref
  1.3 852.2 %sweeps.1 = f32[1536,256]{1,0:T(8,128)} custom-call(bf16[3072,12288]{1,0:T(8,128)(2,1)} %a_ref.1, f32[1536,256]{1,0:T(8,128)} %x_ref.1, f32[1536,256]{1,0:T(8,128)} %v_ref.1, f32[12,128]{1,0:T(8,128)} %convert_bitcast_fusion.dang_ref), custom_call_target="tpu_custom_call" | custom-call | tf_op jit(solution)/shard_map/sweeps/pallas_call | solution.py:553
  853.5 2.7 copy.6

commit v4 on v3

--- a/solution.py
+++ b/solution.py
@@ -7,15 +7,15 @@
 
 SWEEPS = 8
 DAMPING = 0.85
-CH = 32
+CH = 64
 BR = 128
-AHEAD = 4
-TAIL = 4
-RELAY, BACK, BACK_RELAYED, OVER_Y, OVER_Y_RELAYED, OVER_X, OVER_X_RELAYED, HERE, HERE_RELAYED = 4, 6, 10, 10, 14, 14, 17, 16, 19
-DRAIN = 17
-SENT = 20
+AHEAD = 3
+TAIL = 2
+RELAY, BACK, BACK_RELAYED, OVER_Y, OVER_Y_RELAYED, OVER_X, OVER_X_RELAYED, HERE, HERE_RELAYED = 2, 3, 5, 5, 7, 7, 9, 8, 10
+DRAIN = 8
+SENT = 11
 LAG = 2
-FINAL_RELAY = 6
+FINAL_RELAY = 3
 SLOTS = 3
 MT = 512
 MB = 256
@@ -146,21 +146,20 @@
     def block_x(p, q):
         return xbuf[p, q].reshape(8 * BR, vecs)
 
-    def multiply(p, b, g, k):
+    def multiply(p, b, g, turn):
         slot = lax.rem(g, SLOTS)
-
-        @pl.when(k == 0)
+        share = 2 * piece // per
+
+        @pl.when(turn == 0)
         def _():
             landed(abuf.at[slot], a_sem.at[slot])
 
-        x_k = xbuf[p, b, k].reshape(2 * BR, vecs)
-
-        @pl.loop(0, 2 * piece // MT)
+        @pl.loop(0, share // MT)
         def _(m):
-            rows = at(m * MT, MT)
-            yacc[p, rows] += jnp.dot(abuf[slot, rows, at(k * 2 * BR, 2 * BR)], x_k, preferred_element_type=jnp.float32)
-
-        @pl.when(k == 3)
+            rows = at(turn * share + m * MT, MT)
+            yacc[p, rows] += jnp.dot(abuf[slot, rows], block_x(p, b), preferred_element_type=jnp.float32)
+
+        @pl.when(turn == per - 1)
         def _():
             a_next(g)
 
@@ -281,8 +280,9 @@
 
             @pl.when(b < blocks - 1)
             def _():
-                for k in range(4):
-                    multiply(0, b, b, k)
+                @pl.loop(0, per)
+                def _(turn):
+                    multiply(0, b, b, turn)
 
     @pl.when(moves)
     def _():
@@ -449,13 +449,12 @@
             def _():
                 clear(p)
 
-            turn = step - HERE_RELAYED - per // 2
+            turn = step - HERE_RELAYED
             b = turn // per
 
             @pl.when((turn >= 0) & (b < blocks - 1))
             def _():
-                for k in range(4 // per):
-                    multiply(p, b, (sweep + 1) * blocks + b, turn % per * (4 // per) + k)
+                multiply(p, b, (sweep + 1) * blocks + b, turn % per)
 
             q, on = chunk(SENT, lambda q: True)
 

time: 856 us -> 580 us (0.68)
  Pallas kernels: 852 us -> 575 us
    pallas_call x1, Pallas kernels: 852 us -> 575 us  [local_sweeps(): pl.pallas_call(sweeps_kernel, out_shape=jax.ShapeDtypeStruct((piece, vecs...]
where the time goes in v4:
time: 580 us; the launch traced here: 579 us
  Pallas kernels  575 us (99%)
    pallas_call x1, Pallas kernels, local_sweeps(): pl.pallas_call(sweeps_kernel, out_shape=jax.ShapeDtypeStruct((piece, vecs...  575 us

profile of v4, /device:TPU:1, one launch (start us, length us, event | category | flops | bytes accessed | tf_op | source)
XLA Modules:
  0.0 579.1 jit_solution(16773881800981061172)
XLA Ops:
  0.0 1.3 convert_bitcast_fusion.dang_ref
  1.3 575.1 %sweeps.1 = f32[1536,256]{1,0:T(8,128)} custom-call(bf16[3072,12288]{1,0:T(8,128)(2,1)} %a_ref.1, f32[1536,256]{1,0:T(8,128)} %x_ref.1, f32[1536,256]{1,0:T(8,128)} %v_ref.1, f32[12,128]{1,0:T(8,128)} %convert_bitcast_fusion.dang_ref), custom_call_target="tpu_custom_call" | custom-call | tf_op jit(solution)/shard_map/sweeps/pallas_call | solution.py:552
  576.4 2.7 copy.6

commit v5 on v2

v5 whole, which is shorter than its diff:
```python
import jax
import jax.numpy as jnp
from jax import lax
from jax.experimental import pallas as pl
from jax.experimental.pallas import tpu as pltpu
from jax.sharding import PartitionSpec as P

SWEEPS = 8
DAMPING = 0.85
BR = 128
ENDS = 64
WINDOW = 320
SLOTS = 3
MT = 512
MB = 256
LAG = 2
VAHEAD = 3
MESH = pl.DeviceIdType.MESH


def units_of(piece):
    blocks = piece // BR
    units = []
    for b in range(blocks):
        size = ENDS if b == 0 or b >= blocks - 2 else BR
        units += [(row, size, b, b % 2 == 0 and b < blocks - 5) for row in range(b * BR, (b + 1) * BR, size)]
    return units


def plan(piece):
    units = units_of(piece)
    blocks = piece // BR
    waits, ready, arrived = [], {}, 0.5
    for u, (_, size, b, relay) in enumerate(units):
        n = size / 64
        arrived += 1.75 * n
        waits.append((arrived, 'sum', u))
        back = 0.7 * n + 2.4 + (1.5 if b < blocks - 1 else 0.0)
        if relay:
            now = arrived + 0.7 * n + 2.2
            waits.append((now, 'relay', u))
            now += back
            waits.append((now, 'back_relayed', u))
            now += 0.7 * n + 2.2
            waits.append((now, 'over_relayed', u))
        else:
            now = arrived + back
            waits.append((now, 'back', u))
            now += 1.4 * n + 2.2
            waits.append((now, 'over', u))
        now += 1.4 * n + 2.2
        waits.append((now, 'across', u))
        waits.append((now + 6.0, 'sent', u))
        ready[b] = max(ready.get(b, 0.0), now + 1.5)
    waits += [(ready[b], 'here', b) for b in range(blocks - 1)]
    end = ready[blocks - 1]
    waits = sorted(w for w in waits if w[1] != 'sent' or w[0] < end)
    products = [(b, half) for b in range(blocks - 1) for half in range(2)]
    order, now, landed = [], 0.0, set()
    while waits or products:
        free = bool(products) and products[0][0] in landed
        if free and (not waits or now + 0.5 <= waits[0][0]):
            order.append(('product', products.pop(0)))
            now += 0.85
            continue
        when, what, arg = waits.pop(0)
        order.append((what, arg))
        now = max(now, when) + 0.1
        if what == 'here':
            landed.add(arg)
    return order + [('here', blocks - 1)]


def sweeps_kernel(a_ref, x_ref, v_ref, dang_ref, o_ref,
                  abuf, xbuf, xst, rst, yacc, zr, vperm, dperm, dcol, spart, sbuf, svec,
                  a_sem, g_send, gx_recv, gy_recv, gd_recv, gs_recv, v_send, v_recv, dang_sem, o_send, o_recv, f_send, f_recv,
                  z_send, z_recv, r_send, r_recv, t_send, t_recv, y_send, y_recv, x_send, x_recv,
                  d_send, d_recv, s_send, s_recv):
    i = lax.axis_index('row')
    z = lax.axis_index('col')
    y, x, c = i // 4, (i // 2) % 2, i % 2
    me = z * 8 + i
    home = z == y
    away = z != y
    part = jnp.where(home, 0, 1)
    sib_dev = {'col': z, 'row': i + 1 - 2 * c}
    x_dev = {'col': z, 'row': i + 2 - 4 * x}
    y_row = i + 4 - 8 * y
    y_dev = {'col': z, 'row': y_row}
    z_dev = {'col': 1 - z, 'row': i}
    piece, vecs = o_ref.shape
    blocks = piece // BR
    units = units_of(piece)
    vertices = 16 * piece

    def other(off):
        dev = (me + off) % 16
        return {'col': dev // 8, 'row': dev % 8}, dev

    barrier = pltpu.get_barrier_semaphore()

    @pl.loop(1, 16)
    def _(off):
        dev, _ = other(off)
        pl.semaphore_signal(barrier, inc=1, device_id=dev, device_id_type=MESH)

    def remote(src, dst, send, recv, dev):
        return pltpu.make_async_remote_copy(src_ref=src, dst_ref=dst, send_sem=send, recv_sem=recv,
                                            device_id=dev, device_id_type=MESH)

    def same(ref, send, recv, dev):
        return remote(ref, ref, send, recv, dev)

    def landed(ref, sem):
        pltpu.make_async_copy(ref, ref, sem).wait()

    def at(start, size):
        return pl.ds(pl.multiple_of(start, size), size)

    def rows_of(u):
        return pl.ds(units[u][0], units[u][1])

    def in_block(u):
        return pl.ds(units[u][0] % BR, units[u][1])

    def both(p, u, from_x=x):
        return xbuf.at[p, units[u][2], from_x, c, :, in_block(u)]

    def one(p, u, b):
        return xbuf.at[p, units[u][2], x, c, b, in_block(u)]

    def z_copy(t, u):
        start, size = units[u][:2]
        rows = pl.ds(pl.multiple_of((1 - part) * piece + start, ENDS), size)
        return remote(yacc.at[t, rows], zr.at[t, rows_of(u)], z_send.at[t, u], z_recv.at[t, u], z_dev)

    def z_start(t, first, summed):
        while first < len(units) and units[first][0] + units[first][1] <= units[summed][0] + WINDOW:
            z_copy(t, first).start()
            first += 1
        return first

    def r_copy(p, u):
        return remote(xst.at[p, rows_of(u)], one(p, u, 1), r_send.at[p, u], r_recv.at[p, u], z_dev)

    def to_relay(p, u):
        return remote(xst.at[p, rows_of(u)], rst.at[p, rows_of(u)], r_send.at[p, u], t_recv.at[p, u], y_dev)

    def from_relay(p, u):
        return remote(rst.at[p, rows_of(u)], one(p, u, 1), t_send.at[p, u], r_recv.at[p, u], z_dev)

    def y_copy(p, u, ref):
        return same(ref, y_send.at[p, u], y_recv.at[p, u], y_dev)

    def x_copy(p, u):
        return same(both(p, u), x_send.at[p, u], x_recv.at[p, u], x_dev)

    def d_copy(p, b):
        return same(xbuf.at[p, b, :, c], d_send.at[p, b], d_recv.at[p, b], sib_dev)

    def s_copy(p, off):
        dev, _ = other(off)
        return remote(spart.at[p], sbuf.at[p, me], s_send.at[p, off], s_recv.at[p, me], dev)

    def send_s(p):
        sbuf[p, me] = spart[p]

        @pl.loop(1, 16)
        def _(off):
            s_copy(p, off).start()

    def sum_s(t):
        @pl.loop(1, 16)
        def _(off):
            _, dev = other(off)
            landed(sbuf.at[t, dev], s_recv.at[t, dev])

        s_sum = jnp.sum(sbuf[t].reshape(16 * 8, vecs), axis=0, keepdims=True) / vertices
        svec[...] = jnp.broadcast_to(DAMPING * s_sum + (1.0 - DAMPING), svec.shape)

    def a_start(g):
        q = lax.rem(g, blocks)
        slot = lax.rem(g, SLOTS)
        for b in range(8):
            cols = at(b * piece + q * BR, BR)
            pltpu.make_async_copy(a_ref.at[:, cols], abuf.at[slot, :, pl.ds(b * BR, BR)], a_sem.at[slot]).start()

    def a_next(g):
        @pl.when(g + SLOTS < SWEEPS * blocks)
        def _():
            a_start(g + SLOTS)

    def block_x(p, q):
        return xbuf[p, q].reshape(8 * BR, vecs)

    def multiply(p, b, g, turn):
        slot = lax.rem(g, SLOTS)
        share = piece

        @pl.when(turn == 0)
        def _():
            landed(abuf.at[slot], a_sem.at[slot])

        @pl.loop(0, share // MT)
        def _(m):
            rows = at(turn * share + m * MT, MT)
            yacc[p, rows] += jnp.dot(abuf[slot, rows], block_x(p, b), preferred_element_type=jnp.float32)

        @pl.when(turn == 1)
        def _():
            a_next(g)

    ahead = sum(start + size <= MB for start, size, _, _ in units)

    def multiply_last(p, g):
        slot = lax.rem(g, SLOTS)
        landed(abuf.at[slot], a_sem.at[slot])
        x_last = block_x(p, blocks - 1)

        @pl.loop(0, piece // MB)
        def _(m):
            for which in (1 - part, part):
                rows = at(which * piece + m * MB, MB)
                yacc[p, rows] += jnp.dot(abuf[slot, rows], x_last, preferred_element_type=jnp.float32)

            @pl.when(m == 0)
            def _():
                for u in range(ahead):
                    z_copy(p, u).start()

        a_next(g)

    def clear(p):
        @pl.loop(0, 2 * piece // MB)
        def _(m):
            yacc[p, at(m * MB, MB)] = jnp.zeros((MB, vecs), jnp.float32)

    def new_rows(t, u):
        start, size = units[u][:2]
        mine = pl.ds(pl.multiple_of(part * piece + start, ENDS), size)
        landed(zr.at[t, rows_of(u)], z_recv.at[t, u])
        return DAMPING * (yacc[t, mine] + zr[t, rows_of(u)]) + svec[0:1] * vperm[rows_of(u)]

    def dang_sum(col, rows_f32):
        halves = [col * rows_f32[:, h:h + 128] for h in range(0, vecs, 128)]
        return jnp.sum(jnp.concatenate(halves, axis=1).reshape(-1, 8, vecs), axis=0)

    def dang_col(ref, b):
        return jnp.transpose(jnp.broadcast_to(ref[pl.ds(b, 1)], (BR, 128)))

    @pl.loop(0, SLOTS)
    def _(g):
        a_start(g)

    o_p = 2 * i + part
    o_dev = {'col': o_p // 8, 'row': o_p % 8}
    moves = o_p != me
    stays = o_p == me
    v_row = me // 2
    v_dev = {'col': jnp.where(me % 2 == 0, v_row // 4, 1 - v_row // 4), 'row': v_row}

    def v_copy(b):
        rows = at(b * BR, BR)
        return remote(v_ref.at[rows], vperm.at[rows], v_send.at[b], v_recv.at[b], v_dev)

    dang_copy = remote(dang_ref, dperm, dang_sem.at[0], dang_sem.at[1], v_dev)

    spart[0] = jnp.zeros(spart.shape[1:], jnp.float32)

    @pl.loop(0, blocks)
    def _(b):
        rows_x = x_ref[at(b * BR, BR)]
        xbuf[0, b, y, x, c] = rows_x.astype(jnp.bfloat16)
        spart[0] += dang_sum(dang_col(dang_ref, b), rows_x)

    pl.semaphore_wait(barrier, 15)

    @pl.when(moves)
    def _():
        dang_copy.start()

    @pl.when(stays)
    def _():
        dperm[...] = dang_ref[...]
        vperm[...] = v_ref[...]

    send_s(0)
    clear(0)

    @pl.loop(0, blocks + 3 * LAG)
    def _(step):
        @pl.when(step < blocks)
        def _():
            own = xbuf.at[0, step, y, x, c]
            same(own, g_send.at[step], gx_recv.at[step], x_dev).start()
            same(own, g_send.at[step], gy_recv.at[step], y_dev).start()
            same(own, g_send.at[step], gs_recv.at[step], sib_dev).start()

        @pl.when((step >= LAG) & (step < blocks + LAG))
        def _():
            b = step - LAG
            from_x, from_y = xbuf.at[0, b, y, 1 - x, c], xbuf.at[0, b, 1 - y, x, c]
            landed(from_y, gy_recv.at[b])

            @pl.when(b % 2 == 0)
            def _():
                same(from_y, g_send.at[b], gd_recv.at[b], x_dev).start()

            landed(from_x, gx_recv.at[b])

            @pl.when(b % 2 == 1)
            def _():
                same(from_x, g_send.at[b], gd_recv.at[b], y_dev).start()

            same(from_x, g_send.at[b], gs_recv.at[b], sib_dev).start()
            same(from_y, g_send.at[b], gs_recv.at[b], sib_dev).start()

        @pl.when((step >= 2 * LAG) & (step < blocks + 2 * LAG))
        def _():
            b = step - 2 * LAG
            from_d = xbuf.at[0, b, 1 - y, 1 - x, c]
            landed(from_d, gd_recv.at[b])
            same(from_d, g_send.at[b], gs_recv.at[b], sib_dev).start()

        @pl.when(step >= 3 * LAG)
        def _():
            b = step - 3 * LAG
            landed(xbuf.at[0, b, :, :, 1 - c], gs_recv.at[b])

            @pl.when(b < blocks - 1)
            def _():
                @pl.loop(0, 2)
                def _(turn):
                    multiply(0, b, b, turn)

    @pl.when(moves)
    def _():
        for b in range(VAHEAD):
            v_copy(b).start()

    multiply_last(0, blocks - 1)

    @pl.loop(0, blocks)
    def _(b):
        landed(yacc.at[1, pl.ds(0, 7 * BR // 2)], g_send.at[b])

    @pl.loop(1, 16)
    def _(off):
        s_copy(0, off).wait_send()

    @pl.when(moves)
    def _():
        dang_copy.wait()

    @pl.loop(0, blocks)
    def _(b):
        dcol[at(b * BR, BR)] = dang_col(dperm, b)

    @pl.loop(0, SWEEPS - 1)
    def _(sweep):
        t = lax.rem(sweep, 2)
        p = 1 - t
        sum_s(t)
        spart[p] = jnp.zeros(spart.shape[1:], jnp.float32)

        issued = ahead

        def sent(u):
            z_copy(t, u).wait_send()
            x_copy(p, u).wait_send()

            @pl.when(away)
            def _():
                r_copy(p, u).wait_send()

            if units[u][3]:
                y_copy(p, u, one(p, u, part)).wait_send()

                @pl.when(home)
                def _():
                    from_relay(p, u).wait_send()
            else:
                @pl.when(home)
                def _():
                    y_copy(p, u, both(p, u)).wait_send()

        waiting = list(range(len(units)))
        for what, arg in plan(piece):
            u = arg
            if what == 'sum':
                start, size, b, relay = units[u]
                issued = z_start(t, issued, u)
                if start % BR == 0:
                    @pl.when(moves & (sweep == 0))
                    def _(b=b):
                        if b + VAHEAD < blocks:
                            v_copy(b + VAHEAD).start()
                        v_copy(b).wait_recv()

                rows_new = new_rows(t, u)
                rows_bf = rows_new.astype(jnp.bfloat16)

                @pl.when(home)
                def _():
                    xbuf[p, b, x, c, 0, in_block(u)] = rows_bf

                @pl.when(away)
                def _():
                    xst[p, rows_of(u)] = rows_bf

                spart[p] += dang_sum(dcol[rows_of(u)], rows_new)

                @pl.when(away)
                def _():
                    (to_relay if relay else r_copy)(p, u).start()

                if relay:
                    @pl.when(home)
                    def _():
                        y_copy(p, u, one(p, u, 0)).start()
                if u == len(units) - 1:
                    send_s(p)
                if u == 1:
                    clear(p)
            elif what == 'relay':
                @pl.when(home)
                def _():
                    landed(rst.at[p, rows_of(u)], t_recv.at[p, u])
                    from_relay(p, u).start()
            elif what == 'back':
                @pl.when(home)
                def _():
                    landed(one(p, u, 1), r_recv.at[p, u])
                    y_copy(p, u, both(p, u)).start()
                    x_copy(p, u).start()
            elif what == 'over':
                @pl.when(away)
                def _():
                    landed(both(p, u), y_recv.at[p, u])
                    x_copy(p, u).start()
            elif what == 'back_relayed':
                @pl.when(away)
                def _():
                    landed(one(p, u, 1), r_recv.at[p, u])
                    y_copy(p, u, one(p, u, 1)).start()
                    landed(one(p, u, 0), y_recv.at[p, u])
                    x_copy(p, u).start()
            elif what == 'over_relayed':
                @pl.when(home)
                def _():
                    landed(one(p, u, 1), y_recv.at[p, u])
                    x_copy(p, u).start()
            elif what == 'across':
                landed(both(p, u, 1 - x), x_recv.at[p, u])
                if (units[u][0] + units[u][1]) % BR == 0:
                    d_copy(p, units[u][2]).start()
            elif what == 'here':
                landed(xbuf.at[p, arg, :, 1 - c], d_recv.at[p, arg])
            elif what == 'product':
                multiply(p, arg[0], (sweep + 1) * blocks + arg[0], arg[1])
            else:
                waiting.remove(u)
                sent(u)

        multiply_last(p, (sweep + 1) * blocks + blocks - 1)
        for u in waiting:
            sent(u)

        @pl.loop(0, blocks)
        def _(b):
            d_copy(p, b).wait_send()

        @pl.loop(1, 16)
        def _(off):
            s_copy(p, off).wait_send()

    t = (SWEEPS - 1) % 2

    def o_copy(u):
        rows = rows_of(u)
        return remote(zr.at[t, rows], o_ref.at[rows], o_send.at[u], o_recv.at[u], o_dev)

    def o_to_relay(u):
        rows = rows_of(u)
        return remote(zr.at[t, rows], zr.at[1 - t, rows], o_send.at[u], f_recv.at[u], y_dev)

    def o_from_relay(u):
        rows = rows_of(u)
        dev = 2 * y_row + 1
        return remote(zr.at[1 - t, rows], o_ref.at[rows], f_send.at[u], o_recv.at[u],
                      {'col': dev // 8, 'row': dev % 8})

    sum_s(t)
    issued = ahead
    for what, u in [event for event in plan(piece) if event[0] in ('sum', 'relay')]:
        rows = rows_of(u)
        if what == 'sum':
            issued = z_start(t, issued, u)
            rows_new = new_rows(t, u)

            @pl.when(moves)
            def _():
                zr[t, rows] = rows_new

            if units[u][3]:
                @pl.when(away)
                def _():
                    o_to_relay(u).start()

            @pl.when(moves & (home if units[u][3] else home | away))
            def _():
                o_copy(u).start()

            @pl.when(stays)
            def _():
                o_ref[rows] = rows_new
        else:
            @pl.when(home)
            def _():
                landed(zr.at[1 - t, rows], f_recv.at[u])
                o_from_relay(u).start()

    for u in range(len(units)):
        z_copy(t, u).wait_send()

        @pl.when(moves)
        def _():
            o_copy(u).wait()

        if units[u][3]:
            @pl.when(home)
            def _():
                o_from_relay(u).wait_send()

    @pl.when(moves)
    def _():
        @pl.loop(0, blocks)
        def _(b):
            v_copy(b).wait_send()


def solution(mesh):
    def local_sweeps(mat_tile, x_piece, tele_piece, dang_piece):
        piece, vecs = x_piece.shape
        blocks, exchanges = piece // BR, len(units_of(piece))
        dang_rows = dang_piece.astype(jnp.float32).reshape(blocks, 128)
        sems = pltpu.SemaphoreType.DMA
        return pl.pallas_call(
            sweeps_kernel,
            out_shape=jax.ShapeDtypeStruct((piece, vecs), jnp.float32),
            in_specs=[pl.BlockSpec(memory_space=pl.ANY)] + [pl.BlockSpec(memory_space=pltpu.VMEM)] * 3,
            out_specs=pl.BlockSpec(memory_space=pltpu.VMEM),
            scratch_shapes=[
                pltpu.VMEM((SLOTS, 2 * piece, 8 * BR), jnp.bfloat16),
                pltpu.VMEM((2, blocks, 2, 2, 2, BR, vecs), jnp.bfloat16),
                pltpu.VMEM((2, piece, vecs), jnp.bfloat16),
                pltpu.VMEM((2, piece, vecs), jnp.bfloat16),
                pltpu.VMEM((2, 2 * piece, vecs), jnp.float32),
                pltpu.VMEM((2, piece, vecs), jnp.float32),
                pltpu.VMEM((piece, vecs), jnp.float32),
                pltpu.VMEM((blocks, 128), jnp.float32),
                pltpu.VMEM((piece, 128), jnp.float32),
                pltpu.VMEM((2, 8, vecs), jnp.float32),
                pltpu.VMEM((2, 16, 8, vecs), jnp.float32),
                pltpu.VMEM((8, vecs), jnp.float32),
                sems((SLOTS,)),
            ] + [sems((blocks,))] * 7 + [sems((2,))] + [sems((exchanges,))] * 4 + [sems((2, exchanges))] * 10
            + [sems((2, blocks))] * 2
            + [sems((2, 16))] * 2,
            compiler_params=pltpu.CompilerParams(collective_id=0, has_side_effects=True,
                                                 vmem_limit_bytes=67_000_000),
            name='sweeps',
        )(mat_tile, x_piece, tele_piece, dang_rows)

    vec_spec = P(('col', 'row'), None)
    return jax.shard_map(local_sweeps, mesh=mesh,
                         in_specs=(P('row', 'col'), vec_spec, vec_spec, P(('col', 'row'))),
                         out_specs=vec_spec, check_vma=False)
```

time: 588 us -> 640 us (1.088)
  Pallas kernels: 584 us -> 635 us
    pallas_call x1, Pallas kernels: 584 us -> 635 us  [local_sweeps(): pl.pallas_call(sweeps_kernel, out_shape=jax.ShapeDtypeStruct((piece, vecs...]
where the time goes in v5:
time: 640 us; the launch traced here: 639 us
  Pallas kernels  635 us (99%)
    pallas_call x1, Pallas kernels, local_sweeps(): pl.pallas_call(sweeps_kernel, out_shape=jax.ShapeDtypeStruct((piece, vecs...  635 us

profile of v5, /device:TPU:1, one launch (start us, length us, event | category | flops | bytes accessed | tf_op | source)
XLA Modules:
  0.0 638.9 jit_solution(17547355679642908231)
XLA Ops:
  0.0 1.3 convert_bitcast_fusion.dang_ref
  1.3 634.9 %sweeps.1 = f32[1536,256]{1,0:T(8,128)} custom-call(bf16[3072,12288]{1,0:T(8,128)(2,1)} %a_ref.1, f32[1536,256]{1,0:T(8,128)} %x_ref.1, f32[1536,256]{1,0:T(8,128)} %v_ref.1, f32[12,128]{1,0:T(8,128)} %convert_bitcast_fusion.dang_ref), custom_call_target="tpu_custom_call" | custom-call | tf_op jit(solution)/shard_map/sweeps/pallas_call | solution.py:548
  636.3 2.7 copy.6

commit v6 on v4

--- a/solution.py
+++ b/solution.py
@@ -16,16 +16,16 @@
 SENT = 11
 LAG = 2
 FINAL_RELAY = 3
-SLOTS = 3
+SLOTS = 4
 MT = 512
 MB = 256
 VAHEAD = 3
 MESH = pl.DeviceIdType.MESH
 
 
-def sweeps_kernel(a_ref, x_ref, v_ref, dang_ref, o_ref,
+def sweeps_kernel(a_ref, x_ref, v_ref, dang_ref, o_ref, pack_ref,
                   abuf, xbuf, xst, rst, yacc, zr, vperm, dperm, dcol, spart, sbuf, svec,
-                  a_sem, g_send, gx_recv, gy_recv, gd_recv, gs_recv, v_send, v_recv, dang_sem, o_send, o_recv, f_send, f_recv,
+                  a_sem, pack_sem, g_send, gx_recv, gy_recv, gd_recv, gs_recv, v_send, v_recv, dang_sem, o_send, o_recv, f_send, f_recv,
                   z_send, z_recv, r_send, r_recv, t_send, t_recv, y_send, y_recv, x_send, x_recv,
                   d1_send, d1_recv, d2_send, d2_recv, s_send, s_recv):
     i = lax.axis_index('row')
@@ -138,21 +138,42 @@
             cols = at(b * piece + q * BR, BR)
             pltpu.make_async_copy(a_ref.at[:, cols], abuf.at[slot, :, pl.ds(b * BR, BR)], a_sem.at[slot]).start()
 
-    def a_next(g):
-        @pl.when(g + SLOTS < SWEEPS * blocks)
-        def _():
-            a_start(g + SLOTS)
+    def a_packed(g):
+        slot = lax.rem(g, SLOTS)
+        pltpu.make_async_copy(pack_ref.at[lax.rem(g, blocks)], abuf.at[slot], a_sem.at[slot]).start()
+
+    def pack(g):
+        slot = lax.rem(g, SLOTS)
+        return pltpu.make_async_copy(abuf.at[slot], pack_ref.at[g], pack_sem.at[slot])
+
+    def a_next(g, first):
+        if first:
+            pack(g).wait()
+
+            @pl.when(g + SLOTS < blocks)
+            def _():
+                a_start(g + SLOTS)
+
+            @pl.when(g + SLOTS >= blocks)
+            def _():
+                a_packed(g + SLOTS)
+        else:
+            @pl.when(g + SLOTS < SWEEPS * blocks)
+            def _():
+                a_packed(g + SLOTS)
 
     def block_x(p, q):
         return xbuf[p, q].reshape(8 * BR, vecs)
 
-    def multiply(p, b, g, turn):
+    def multiply(p, b, g, turn, first=False):
         slot = lax.rem(g, SLOTS)
         share = 2 * piece // per
 
         @pl.when(turn == 0)
         def _():
             landed(abuf.at[slot], a_sem.at[slot])
+            if first:
+                pack(g).start()
 
         @pl.loop(0, share // MT)
         def _(m):
@@ -161,11 +182,13 @@
 
         @pl.when(turn == per - 1)
         def _():
-            a_next(g)
-
-    def multiply_last(p, g):
+            a_next(g, first)
+
+    def multiply_last(p, g, first=False):
         slot = lax.rem(g, SLOTS)
         landed(abuf.at[slot], a_sem.at[slot])
+        if first:
+            pack(g).start()
         x_last = block_x(p, blocks - 1)
 
         @pl.loop(0, piece // MB)
@@ -179,7 +202,7 @@
                 for q in range(AHEAD):
                     z_copy(p, q).start()
 
-        a_next(g)
+        a_next(g, first)
 
     def clear(p):
         @pl.loop(0, 2 * piece // MB)
@@ -282,14 +305,14 @@
             def _():
                 @pl.loop(0, per)
                 def _(turn):
-                    multiply(0, b, b, turn)
+                    multiply(0, b, b, turn, first=True)
 
     @pl.when(moves)
     def _():
         for b in range(VAHEAD):
             v_copy(b).start()
 
-    multiply_last(0, blocks - 1)
+    multiply_last(0, blocks - 1, first=True)
 
     @pl.loop(0, blocks)
     def _(b):
@@ -549,11 +572,12 @@
         chunks, blocks = piece // CH, piece // BR
         dang_rows = dang_piece.astype(jnp.float32).reshape(blocks, 128)
         sems = pltpu.SemaphoreType.DMA
-        return pl.pallas_call(
+        out, _ = pl.pallas_call(
             sweeps_kernel,
-            out_shape=jax.ShapeDtypeStruct((piece, vecs), jnp.float32),
+            out_shape=(jax.ShapeDtypeStruct((piece, vecs), jnp.float32),
+                       jax.ShapeDtypeStruct((blocks, 2 * piece, 8 * BR), jnp.bfloat16)),
             in_specs=[pl.BlockSpec(memory_space=pl.ANY)] + [pl.BlockSpec(memory_space=pltpu.VMEM)] * 3,
-            out_specs=pl.BlockSpec(memory_space=pltpu.VMEM),
+            out_specs=(pl.BlockSpec(memory_space=pltpu.VMEM), pl.BlockSpec(memory_space=pl.ANY)),
             scratch_shapes=[
                 pltpu.VMEM((SLOTS, 2 * piece, 8 * BR), jnp.bfloat16),
                 pltpu.VMEM((2, blocks, 4, 2, BR, vecs), jnp.bfloat16),
@@ -567,7 +591,7 @@
                 pltpu.VMEM((2, 8, vecs), jnp.float32),
                 pltpu.VMEM((2, 16, 8, vecs), jnp.float32),
                 pltpu.VMEM((8, vecs), jnp.float32),
-                sems((SLOTS,)),
+                sems((SLOTS,)), sems((SLOTS,)),
             ] + [sems((blocks,))] * 7 + [sems((2,))] + [sems((chunks,))] * 4 + [sems((2, chunks))] * 4
             + [sems((2, chunks // 2))] * 2 + [sems((2, chunks))] * 8
             + [sems((2, 16))] * 2,
@@ -575,6 +599,7 @@
                                                  vmem_limit_bytes=67_000_000),
             name='sweeps',
         )(mat_tile, x_piece, tele_piece, dang_rows)
+        return out
 
     vec_spec = P(('col', 'row'), None)
     return jax.shard_map(local_sweeps, mesh=mesh,

time: 580 us -> 590 us (1.017)
  Pallas kernels: 575 us -> 586 us
    pallas_call x1, Pallas kernels: 575 us -> 586 us  [local_sweeps(): pl.pallas_call(sweeps_kernel, out_shape=(jax.ShapeDtypeStruct((piece, vec...]
where the time goes in v6:
time: 590 us
  Pallas kernels  586 us (99%)
    pallas_call x1, Pallas kernels, local_sweeps(): pl.pallas_call(sweeps_kernel, out_shape=(jax.ShapeDtypeStruct((piece, vec...  586 us

profile of v6, /device:TPU:1, one launch (start us, length us, event | category | flops | bytes accessed | tf_op | source)
XLA Modules:
  0.0 590.2 jit_solution(7244043812019965087)
XLA Ops:
  0.0 1.3 convert_bitcast_fusion.dang_ref
  1.3 586.3 %sweeps.1 = (f32[1536,256]{1,0:T(8,128)}, bf16[12,3072,1024]{2,1,0:T(8,128)(2,1)}) custom-call(bf16[3072,12288]{1,0:T(8,128)(2,1)} %a_ref.1, f32[1536,256]{1,0:T(8,128)} %x_ref.1, f32[1536,256]{1,0:T(8,128)} %v_ref.1, f32[12,128]{1,0:T(8,128)} %convert_bitcast_fusion.dang_ref), custom_call_target="tpu_custom_call" | custom-call | tf_op jit(solution)/shard_map/sweeps/pallas_call | solution.py:575
  587.6 2.7 copy.6

commit v7 on v4

--- a/solution.py
+++ b/solution.py
@@ -9,7 +9,7 @@
 DAMPING = 0.85
 CH = 64
 BR = 128
-AHEAD = 3
+AHEAD = 4
 TAIL = 2
 RELAY, BACK, BACK_RELAYED, OVER_Y, OVER_Y_RELAYED, OVER_X, OVER_X_RELAYED, HERE, HERE_RELAYED = 2, 3, 5, 5, 7, 7, 9, 8, 10
 DRAIN = 8
@@ -143,6 +143,8 @@
         def _():
             a_start(g + SLOTS)
 
+    used = pl.ds(0, 8 * BR)
+
     def block_x(p, q):
         return xbuf[p, q].reshape(8 * BR, vecs)
 
@@ -152,12 +154,12 @@
 
         @pl.when(turn == 0)
         def _():
-            landed(abuf.at[slot], a_sem.at[slot])
+            landed(abuf.at[slot, :, used], a_sem.at[slot])
 
         @pl.loop(0, share // MT)
         def _(m):
             rows = at(turn * share + m * MT, MT)
-            yacc[p, rows] += jnp.dot(abuf[slot, rows], block_x(p, b), preferred_element_type=jnp.float32)
+            yacc[p, rows] += jnp.dot(abuf[slot, rows, used], block_x(p, b), preferred_element_type=jnp.float32)
 
         @pl.when(turn == per - 1)
         def _():
@@ -165,14 +167,14 @@
 
     def multiply_last(p, g):
         slot = lax.rem(g, SLOTS)
-        landed(abuf.at[slot], a_sem.at[slot])
+        landed(abuf.at[slot, :, used], a_sem.at[slot])
         x_last = block_x(p, blocks - 1)
 
         @pl.loop(0, piece // MB)
         def _(m):
             for which in (1 - part, part):
                 rows = at(which * piece + m * MB, MB)
-                yacc[p, rows] += jnp.dot(abuf[slot, rows], x_last, preferred_element_type=jnp.float32)
+                yacc[p, rows] += jnp.dot(abuf[slot, rows, used], x_last, preferred_element_type=jnp.float32)
 
             @pl.when(m == 0)
             def _():
@@ -555,7 +557,7 @@
             in_specs=[pl.BlockSpec(memory_space=pl.ANY)] + [pl.BlockSpec(memory_space=pltpu.VMEM)] * 3,
             out_specs=pl.BlockSpec(memory_space=pltpu.VMEM),
             scratch_shapes=[
-                pltpu.VMEM((SLOTS, 2 * piece, 8 * BR), jnp.bfloat16),
+                pltpu.VMEM((SLOTS, 2 * piece, 9 * BR), jnp.bfloat16),
                 pltpu.VMEM((2, blocks, 4, 2, BR, vecs), jnp.bfloat16),
                 pltpu.VMEM((2, chunks, CH, vecs), jnp.bfloat16),
                 pltpu.VMEM((2, chunks // 2, CH, vecs), jnp.bfloat16),

time: 580 us -> 588 us (1.014)
  Pallas kernels: 575 us -> 582 us
    pallas_call x1, Pallas kernels: 575 us -> 582 us  [local_sweeps(): pl.pallas_call(sweeps_kernel, out_shape=jax.ShapeDtypeStruct((piece, vecs...]
where the time goes in v7:
time: 588 us; the launch traced here: 586 us
  Pallas kernels  582 us (99%)
    pallas_call x1, Pallas kernels, local_sweeps(): pl.pallas_call(sweeps_kernel, out_shape=jax.ShapeDtypeStruct((piece, vecs...  582 us

profile of v7, /device:TPU:1, one launch (start us, length us, event | category | flops | bytes accessed | tf_op | source)
XLA Modules:
  0.0 585.6 jit_solution(3403327236479621769)
XLA Ops:
  0.0 1.3 convert_bitcast_fusion.dang_ref
  1.3 581.7 %sweeps.1 = f32[1536,256]{1,0:T(8,128)} custom-call(bf16[3072,12288]{1,0:T(8,128)(2,1)} %a_ref.1, f32[1536,256]{1,0:T(8,128)} %x_ref.1, f32[1536,256]{1,0:T(8,128)} %v_ref.1, f32[12,128]{1,0:T(8,128)} %convert_bitcast_fusion.dang_ref), custom_call_target="tpu_custom_call" | custom-call | tf_op jit(solution)/shard_map/sweeps/pallas_call | solution.py:554
  583.0 2.7 copy.6
